TPU v7x, 8 devices: a whole 2x2x1 slice. The times are simulated.
8 devices in a mesh: ey: 2 (over z, y), ex: 4 (over x, core).
Axes of the slice: x: 2, y: 2, z: 1, core: 2. Of those that a mesh axis runs over, the one named last changes fastest.
Arguments:
- x: bfloat16 [1024, 2048], P(('ey', 'ex'))
- kv_k: bfloat16 [1024, 512, 1, 128], P(('ey', 'ex'))
- kv_v: bfloat16 [1024, 512, 1, 128], P(('ey', 'ex'))
- lens: int32 [1024], P(('ey', 'ex'))
- topk_idx: int32 [1024, 6], P(('ey', 'ex'))
- gates: float32 [1024, 6], P(('ey', 'ex'))
- ln1: bfloat16 [2048], replicated
- ln2: bfloat16 [2048], replicated
- wq: bfloat16 [2048, 2048], replicated
- wo: bfloat16 [2048, 2048], replicated
- ws1: bfloat16 [2048, 1408], replicated
- ws3: bfloat16 [2048, 1408], replicated
- ws2: bfloat16 [1408, 2048], replicated
- w1: bfloat16 [64, 2048, 1408], P(('ey', 'ex'))
- w3: bfloat16 [64, 2048, 1408], P(('ey', 'ex'))
- w2: bfloat16 [64, 1408, 2048], P(('ey', 'ex'))
Outputs:
- output: bfloat16 [1024, 2048], P(('ey', 'ex'))
All inputs are finite; a program needn't handle non-finite values.
Results may differ from a plain program's by a relative error of at most 0.0124533.
Values are sent between devices in bfloat16 or wider.
A program may use at most 1 GiB of HBM per device.

v0:
```python
import jax
import jax.numpy as jnp
from jax import lax
from jax.sharding import PartitionSpec as P

EPS = 1e-6
BF = jnp.bfloat16
F32 = jnp.float32


def _rms(v, w):
    v = v.astype(F32)
    r = lax.rsqrt(jnp.mean(v * v, axis=-1, keepdims=True) + EPS)
    return (v * r * w.astype(F32)).astype(BF)


def _ffn(u, w1, w3, w2):
    g = jnp.dot(u, w1, preferred_element_type=F32)
    v = jnp.dot(u, w3, preferred_element_type=F32)
    z = (jax.nn.silu(g) * v).astype(BF)
    return jnp.dot(z, w2, preferred_element_type=F32).astype(BF)


def _experts(xin, w1, w3, w2):
    g = jnp.einsum('erd,edf->erf', xin, w1, preferred_element_type=F32)
    v = jnp.einsum('erd,edf->erf', xin, w3, preferred_element_type=F32)
    z = (jax.nn.silu(g) * v).astype(BF)
    return jnp.einsum('erf,efd->erd', z, w2, preferred_element_type=F32).astype(BF)


def _attn(x, kk, vv, lens, ln1, wq, wo):
    b, l, kvh, dh = kk.shape
    hq = wq.shape[1] // dh
    a = _rms(x, ln1)
    q = jnp.dot(a, wq, preferred_element_type=F32).astype(BF).reshape(b, kvh, hq // kvh, dh)
    s = jnp.einsum('bkgd,blkd->bkgl', q, kk, preferred_element_type=F32) * dh ** -0.5
    valid = jnp.arange(l)[None, :] < lens[:, None]
    s = jnp.where(valid[:, None, None, :], s, -jnp.inf)
    p = jax.nn.softmax(s, axis=-1).astype(BF)
    o = jnp.einsum('bkgl,blkd->bkgd', p, vv, preferred_element_type=F32).astype(BF)
    attn = jnp.dot(o.reshape(b, hq * dh), wo, preferred_element_type=F32)
    return (x.astype(F32) + attn).astype(BF)


def _ranks(topk, n_exp):
    chosen = (topk[..., None] == jnp.arange(n_exp)).any(axis=-2).astype(jnp.int32)
    before = jnp.cumsum(chosen, axis=-2) - chosen
    return jnp.take_along_axis(before, topk, axis=-1)


def solution(mesh):
    ey, ex = mesh.shape['ey'], mesh.shape['ex']
    ndev = ey * ex
    rows = P(('ey', 'ex'))
    rep = P()

    def local(x, kv_k, kv_v, lens, topk_idx, gates, ln1, ln2, wq, wo, ws1, ws3, ws2, w1, w3, w2):
        b, d = x.shape
        k = topk_idx.shape[1]
        edev = w1.shape[0]
        n_exp = edev * ndev
        cap = max(4, (2 * b * k + n_exp - 1) // n_exp)
        nslotv = ex * edev * ey * cap
        iy = lax.axis_index('ey')

        h = _attn(x, kv_k, kv_v, lens, ln1, wq, wo)
        u = _rms(h, ln2)

        u_g = lax.all_gather(u, 'ey')
        t_g = lax.all_gather(topk_idx, 'ey')
        g_g = lax.all_gather(gates, 'ey')

        rank = _ranks(t_g, n_exp)
        mine = (t_g // (edev * ex) == iy) & (rank < cap)
        src = jnp.arange(ey, dtype=jnp.int32)[:, None, None]
        dest = ((t_g // edev) % ex) * edev + t_g % edev
        pos = jnp.where(mine, (dest * ey + src) * cap + rank, nslotv).reshape(-1)
        tok = jnp.broadcast_to(jnp.arange(ey * b, dtype=jnp.int32).reshape(ey, b, 1), t_g.shape).reshape(-1)
        slot_tok = jnp.full((nslotv,), ey * b, jnp.int32).at[pos].set(tok, mode='drop')
        slot_gate = jnp.zeros((nslotv,), F32).at[pos].set(g_g.reshape(-1), mode='drop')
        u_pad = jnp.concatenate([u_g.reshape(ey * b, d), jnp.zeros((1, d), BF)], axis=0)

        send = u_pad[slot_tok].reshape(ex, edev, ey * cap, d)
        recv = lax.all_to_all(send, 'ex', 0, 0)
        xin = recv.transpose(1, 0, 2, 3).reshape(edev, ex * ey * cap, d)
        out = _experts(xin, w1, w3, w2)
        back = out.reshape(edev, ex, ey * cap, d).transpose(1, 0, 2, 3)
        ret = lax.all_to_all(back, 'ex', 0, 0).reshape(nslotv, d)

        partial = jnp.zeros((ey * b + 1, d), F32).at[slot_tok].add(slot_gate[:, None] * ret.astype(F32))
        routed = lax.psum_scatter(partial[: ey * b].reshape(ey, b, d), 'ey', scatter_dimension=0)
        y = h.astype(F32) + _ffn(u, ws1, ws3, ws2).astype(F32) + routed
        return y.astype(BF)

    return jax.shard_map(
        local, mesh=mesh,
        in_specs=(rows, rows, rows, rows, rows, rows, rep, rep, rep, rep, rep, rep, rep, rows, rows, rows),
        out_specs=rows, check_vma=False)
```

profile of v0, /device:TPU:0, one launch (start us, length us, event | category | flops | bytes accessed | tf_op | source)
XLA Modules:
  0.0 368.7 jit_solution(2632209658974236957)
XLA Ops:
  8.5 4.9 %fusion.25 = bf16[16,8,16,128]{3,1,2,0:T(8,128)(2,1)S(1)} fusion(bf16[2048,2048]{1,0:T(8,128)(2,1)} %param.24, bf16[128,2048]{1,0:T(8,128)(2,1)} %param.16, f32[2048]{0:T(1024)S(1)} %convert_element_type.62, f32[128]{0:T(128)S(1)} %add_rsqrt_fusion.1), kind=kOutput, calls=%fused_computation.40 | convolution fusion | flops 1075052544 | bytes 9445888 | tf_op jit(solution)/shard_map/dot_general | solution.py:35
  13.6 12.2 %fusion.3 = f32[128,16,512]{2,1,0:T(8,128)} fusion(bf16[128,16,128]{2,1,0:T(8,128)(2,1)S(1)} %bitcast.69, bf16[128,512,1,128]{3,1,2,0:T(8,128)(2,1)} %param.17), kind=kOutput, calls=%fused_computation.8 | convolution fusion | flops 268435456 | bytes 21495808 | tf_op jit(solution)/shard_map/bkgd,blkd->bkgl/dot_general | solution.py:36
  25.8 5.4 %fusion.59 = (f32[128,16]{1,0:T(8,128)S(1)}, f32[128,16,512]{2,1,0:T(8,128)S(1)}) fusion(f32[128,16,512]{2,1,0:T(8,128)} %fusion.3, pred[128,512]{1,0:T(8,128)(4,1)S(1)} %iota_compare_fusion.1), kind=kOutput, calls=%fused_computation.98 | output fusion | flops 6291967 | bytes 8462336 | tf_op jit(solution)/shard_map/sub | solution.py:39
  31.2 7.3 %fusion.22 = bf16[128,16,128]{2,1,0:T(8,128)(2,1)S(1)} fusion(bf16[128,512,1,128]{3,1,2,0:T(8,128)(2,1)} %param.18, f32[128,16,512]{2,1,0:T(8,128)S(1)} %get-tuple-element.6, f32[128,16]{1,0:T(8,128)S(1)} %get-tuple-element.5), kind=kOutput, calls=%fused_computation.39 | convolution fusion | flops 270794752 | bytes 21504000 | tf_op jit(solution)/shard_map/bkgl,blkd->bkgd/dot_general | solution.py:40
  38.6 1.5 multiply_reduce_fusion
  41.1 5.7 %all-gather = s32[256,6]{0,1:T(8,128)S(1)} all-gather(s32[128,6]{0,1:T(8,128)S(1)} %copy-done.3), channel_id=2, replica_groups=mesh['ey'=2,'ex'=4] {'ey'}, dimensions={0}, use_global_device_ids=true | all-gather | bytes 9216 | tf_op jit(solution)/shard_map/all_gather | solution.py:70
  47.6 12.6 %gather_fusion.1 = s32[1536]{0:T(1024)S(1)} fusion(s32[2,128,64]{2,1,0:T(8,128)S(1)} %convert_subtract_fusion, s32[1536]{0:T(1024)S(1)} %reshape.181), kind=kCustom, calls=%fused_computation.1 | custom fusion | bytes 30720 | tf_op jit(solution)/shard_map/jit(take_along_axis)/gather | solution.py:48
  61.2 6.4 %scatter_custom_fusion = s32[1536]{0:T(1024)S(1)} fusion(s32[1536]{0:T(1024)S(1)} %fusion.50, s32[1536]{0:T(1024)S(1)} %reshape.191, s32[]{:T(128)} %constant.90.clone.1), kind=kCustom, calls=%fused_computation.89 | custom fusion | bytes 6148 | tf_op jit(solution)/shard_map/scatter | solution.py:79
  68.9 7.1 %gather_fusion = bf16[1536,2048]{1,0:T(8,128)(2,1)} fusion(bf16[257,2048]{1,0:T(8,128)(2,1)S(1)} %concatenate.3, s32[2048]{0:T(1024)S(1)} %pad_clamp_fusion), kind=kCustom, calls=%fused_computation | custom fusion | bytes 12589056 | tf_op jit(solution)/shard_map/gather | solution.py:83
  76.0 74.3 %all_to_all.10 = bf16[4,8,48,2048]{3,2,1,0:T(8,128)(2,1)S(1)} all-to-all(bf16[4,8,48,2048]{3,2,1,0:T(8,128)(2,1)} %bitcast.59), channel_id=1, replica_groups=mesh['ey'=2,'ex'=4] {'ex'}, dimensions={0} | all-to-all | bytes 12582912 | tf_op jit(solution)/shard_map/all_to_all | solution.py:84
  150.3 3.3 copy.32
  153.6 22.2 %fusion.61 = f32[8,192,1408]{2,1,0:T(8,128)} fusion(bf16[8,192,2048]{2,1,0:T(8,128)(2,1)} %bitcast.63, bf16[8,2048,1408]{2,1,0:T(8,128)(2,1)} %param.29), kind=kOutput, calls=%fused_computation.100 | convolution fusion | flops 8858370048 | bytes 61079552 | tf_op jit(solution)/shard_map/erd,edf->erf/dot_general | solution.py:25
  175.8 25.2 %multiply_convert_fusion.clone.6 = bf16[8,192,1408]{2,1,0:T(8,128)(2,1)} fusion(f32[8,192,1408]{2,1,0:T(8,128)} %fusion.61, bf16[8,192,2048]{2,1,0:T(8,128)(2,1)} %bitcast.64, bf16[8,2048,1408]{2,1,0:T(8,128)(2,1)} %param.30), kind=kOutput, calls=%fused_computation.12.clone.clone.clone.clone.clone.1 | convolution fusion | flops 8871346176 | bytes 65404928 | tf_op jit(solution)/shard_map/erd,edf->erf/dot_general | solution.py:26
  201.0 18.7 %fusion.8 = bf16[8,192,2048]{2,1,0:T(8,128)(2,1)S(1)} fusion(bf16[8,1408,2048]{2,1,0:T(8,128)(2,1)} %param.31, bf16[8,192,1408]{2,1,0:T(8,128)(2,1)} %multiply_convert_fusion.clone.6), kind=kOutput, calls=%fused_computation.16 | convolution fusion | flops 8861515776 | bytes 56754176 | tf_op jit(solution)/shard_map/erf,efd->erd/dot_general | solution.py:28
  219.7 3.2 copy.43
  222.9 5.4 %all-to-all-start.1 = ((bf16[4,8,48,2048]{3,2,1,0:T(8,128)(2,1)}), bf16[4,8,48,2048]{3,2,1,0:T(8,128)(2,1)}, u32[]{:S(2)}, u32[]{:S(2)}) async-start(bf16[4,8,48,2048]{3,2,1,0:T(8,128)(2,1)} %bitcast.57), calls=%async_computation.1 | async-start | bytes 12582912 | tf_op jit(solution)/shard_map/all_to_all | solution.py:88
  228.3 4.3 %all-gather.1 = f32[256,6]{0,1:T(8,128)S(1)} all-gather(f32[128,6]{0,1:T(8,128)S(1)} %copy-done.4), channel_id=3, replica_groups=mesh['ey'=2,'ex'=4] {'ey'}, dimensions={0}, use_global_device_ids=true | all-gather | bytes 9216 | tf_op jit(solution)/shard_map/all_gather | solution.py:71
  233.0 6.4 %scatter_custom_fusion.1 = f32[1536]{0:T(1024)S(1)} fusion(s32[1536]{0:T(1024)S(1)} %fusion.50, f32[1536]{0:T(1024)S(1)} %reshape.199, f32[]{:T(128)} %constant.84.clone.1), kind=kCustom, calls=%fused_computation.87 | custom fusion | bytes 6148 | tf_op jit(solution)/shard_map/scatter | solution.py:80
  239.4 59.3 %all-to-all-done.1 = bf16[4,8,48,2048]{3,2,1,0:T(8,128)(2,1)} async-done(((bf16[4,8,48,2048]{3,2,1,0:T(8,128)(2,1)}), bf16[4,8,48,2048]{3,2,1,0:T(8,128)(2,1)}, u32[]{:S(2)}, u32[]{:S(2)}) %all-to-all-start.1) | async-done | bytes 6291488 | tf_op jit(solution)/shard_map/all_to_all | solution.py:88
  298.6 23.0 %scatter_custom_fusion.2 = f32[257,2048]{1,0:T(8,128)} fusion(s32[1536]{0:T(1024)S(1)} %compare_select_fusion.1, bf16[1536,2048]{1,0:T(8,128)(2,1)} %bitcast.12, f32[1536]{0:T(1024)S(1)} %scatter_custom_fusion.1, f32[]{:T(128)} %constant.84.clone.1), kind=kCustom, calls=%fused_computation.11 | custom fusion | flops 9437184 | bytes 8404996 | tf_op jit(solution)/shard_map/scatter-add | solution.py:90
  321.6 3.2 slice.9
  324.8 3.6 fusion.60
  328.5 26.1 %reduce-scatter.2.cloned.1.call-done = f32[1,128,2048]{2,1,0:T(8,128)} async-done(((f32[2,128,2048]{2,1,0:T(8,128)}), f32[1,128,2048]{2,1,0:T(8,128)}) %reduce-scatter.2.cloned.1.call-update) | async-done | bytes 1048592 | tf_op jit(solution)/shard_map/reduce_scatter | solution.py:91
  354.6 7.3 %fusion.17 = bf16[128,2048]{1,0:T(8,128)(2,1)} fusion(f32[128,2048]{1,0:T(8,128)S(1)} %get-tuple-element.8, bf16[1408,2048]{1,0:T(8,128)(2,1)} %param.28, f32[1,128,2048]{2,1,0:T(8,128)} %reduce-scatter.2.cloned.1.call-done, bf16[128,2048]{1,0:T(8,128)(2,1)S(1)} %copy-done, bf16[2048,1408]{1,0:T(8,128)(2,1)} %param.27, f32[128,1408]{1,0:T(8,128)S(1)} %fusion.60), kind=kOutput, calls=%fused_computation.32 | convolution fusion | flops 1478787072 | bytes 15400960 | tf_op jit(solution)/shard_map/dot_general | solution.py:21
  (51 shorter events, 6.4 us)
Async XLA Ops:
  6.5 61.0 %all-gather.5.cloned.1.call-start = ((), (), s32[]{:S(2)}) async-start(), calls=%async_computation.4 | async-start | bytes 1572864 | tf_op jit(solution)/shard_map/all_gather | solution.py:69
  8.5 5.0 %copy-start.5 = (s32[128]{0:T(128)S(1)}, s32[128]{0:T(128)}, u32[]{:S(2)}) copy-start(s32[128]{0:T(128)} %param.19) | copy-start | bytes 1540
  25.8 12.8 %slice-start = ((s8[8388608]{0:T(1024)(128)(4,1)}), s8[4194304]{0:T(1024)(128)(4,1)S(1)}, s32[]{:S(2)}) async-start(s8[8388608]{0:T(1024)(128)(4,1)} %bitcast.60), calls=%async_computation.5 | async-start | bytes 8388608
  31.2 7.4 %slice-start.1 = ((s8[8388608]{0:T(1024)(128)(4,1)}), s8[4194304]{0:T(1024)(128)(4,1)S(1)}, s32[]{:S(2)}) async-start(s8[8388608]{0:T(1024)(128)(4,1)} %bitcast.60), calls=%async_computation.6 | async-start | bytes 8388608
  31.2 7.4 %copy-start.1 = (bf16[128,2048]{1,0:T(8,128)(2,1)S(1)}, bf16[128,2048]{1,0:T(8,128)(2,1)}, u32[]{:S(2)}) copy-start(bf16[128,2048]{1,0:T(8,128)(2,1)} %param.16) | copy-start | bytes 1572868
  38.6 1.5 copy-start.2
  38.6 2.5 copy-start.3
  222.9 5.4 %copy-start.4 = (f32[128,6]{0,1:T(8,128)S(1)}, f32[128,6]{0,1:T(8,128)}, u32[]{:S(2)}) copy-start(f32[128,6]{0,1:T(8,128)} %param.21) | copy-start | bytes 9220
  222.9 75.7 %all-to-all-start.1 = ((bf16[4,8,48,2048]{3,2,1,0:T(8,128)(2,1)}), bf16[4,8,48,2048]{3,2,1,0:T(8,128)(2,1)}, u32[]{:S(2)}, u32[]{:S(2)}) async-start(bf16[4,8,48,2048]{3,2,1,0:T(8,128)(2,1)} %bitcast.57), calls=%async_computation.1 | async-start | bytes 12582912 | tf_op jit(solution)/shard_map/all_to_all | solution.py:88
  228.3 126.3 %reduce-scatter.2.cloned.1.call-start = ((), (), s32[]{:S(2)}) async-start(), calls=%async_computation.3 | async-start | bytes 3145728 | tf_op jit(solution)/shard_map/reduce_scatter | solution.py:91
  298.6 26.2 %copy-start = (bf16[128,2048]{1,0:T(8,128)(2,1)S(1)}, bf16[128,2048]{1,0:T(8,128)(2,1)}, u32[]{:S(2)}) copy-start(bf16[128,2048]{1,0:T(8,128)(2,1)} %multiply_convert_fusion.1) | copy-start | bytes 1572868
Sparse Core Ops, SparseCore 0:
  41.2 21.0 all-gather.4
  324.9 29.5 reduce-scatter.1
where the time goes:
time: 369 us
  matrix products  103 us (28%)
  waiting for transfers between devices  85.4 us (23%)
  blocking collectives  84.4 us (23%)
  local copies, waits for them, and re-layouts  44.9 us (12%)
  other arithmetic  32 us (9%)
  between operations  13.8 us (4%)
  starting transfers between devices  5.41 us (1%)
    all_to_all x1, blocking collectives, local(): recv = lax.all_to_all(send, 'ex', 0, 0)  74.3 us
    all_to_all x1, waiting for transfers between devices, local(): ret = lax.all_to_all(back, 'ex', 0, 0).reshape(nslotv, d)  59.3 us
    reduce_scatter x1, waiting for transfers between devices, local(): lax.psum_scatter(partial[:ey * b].reshape(ey, b, d), 'ey', scatter_dimens...  26.1 us
    dot_general x1, matrix products, _experts(): v = jnp.einsum('erd,edf->erf', xin, w3, preferred_element_type=F32)  25.2 us
    scatter-add x1, other arithmetic, local(): jnp.zeros((ey * b + 1, d), F32).at[slot_tok]  23 us
    dot_general x1, matrix products, _experts(): g = jnp.einsum('erd,edf->erf', xin, w1, preferred_element_type=F32)  22.2 us
    dot_general x1, matrix products, _experts(): jnp.einsum('erf,efd->erd', z, w2, preferred_element_type=F32).astype(BF)  18.7 us
    gather x3, local copies, waits for them, and re-layouts, _ranks(): return jnp.take_along_axis(before, topk, axis=-1)  12.9 us
  transfers between devices with their start and end apart: 3, of which 2 were waited for; matrix products, arithmetic and copies ran while one was open for 8% of the time, Pallas kernels for 0%

commit v1 on v0

v1 whole, which is shorter than its diff:
```python
import functools

import jax
import jax.numpy as jnp
from jax import lax
from jax.experimental import pallas as pl
from jax.experimental.pallas import tpu as pltpu
from jax.sharding import PartitionSpec as P

EPS = 1e-6
BF = jnp.bfloat16
F32 = jnp.float32
MESH = pl.DeviceIdType.MESH

NA = 3
NB = 5
NC = 256


def _rms(v, w):
    v = v.astype(F32)
    r = lax.rsqrt(jnp.mean(v * v, axis=-1, keepdims=True) + EPS)
    return (v * r * w.astype(F32)).astype(BF)


def _attn(x, kk, vv, lens, ln1, wq, wo):
    b, l, kvh, dh = kk.shape
    hq = wq.shape[1] // dh
    a = _rms(x, ln1)
    q = jnp.dot(a, wq, preferred_element_type=F32).astype(BF).reshape(b, kvh, hq // kvh, dh)
    s = jnp.einsum('bkgd,blkd->bkgl', q, kk, preferred_element_type=F32) * dh ** -0.5
    valid = jnp.arange(l)[None, :] < lens[:, None]
    s = jnp.where(valid[:, None, None, :], s, -jnp.inf)
    p = jax.nn.softmax(s, axis=-1).astype(BF)
    o = jnp.einsum('bkgl,blkd->bkgd', p, vv, preferred_element_type=F32).astype(BF)
    attn = jnp.dot(o.reshape(b, hq * dh), wo, preferred_element_type=F32)
    return (x.astype(F32) + attn).astype(BF)


def _moe_kernel(dims, u_ref, h_ref, rt_ref, ws1, ws3, ws2, w1, w3, w2, y_ref,
                ug, rt, acc, z, xin, s1h, pg, ring_a, ring_b, fb, acc_s, z_s, base, hv, sib, r_d, r_a, r_b,
                keys, gts, loc_sem, a_sem, b_sem, ag_s, ag_r, fw_s, fw_r, rt_s, rt_r, sb_s, sb_r,
                rd_s, rd_r, ra_s, ra_r, rb_s, rb_r):
    b, d, f, edev, cap, ny, nx, kc, nk, nn = dims
    rows = 8 * cap
    half = 2 * cap
    y = lax.axis_index('ey')
    ex = lax.axis_index('ex')
    x = ex // 2
    c = ex % 2
    me = y * nx + ex
    peers = [(y, 2 * (1 - x) + c), (1 - y, 2 * x + c), (1 - y, 2 * (1 - x) + c), (y, 2 * x + 1 - c)]
    pa = ((1 - c) * y + c * (1 - y), 2 * ((1 - c) * (1 - x) + c * x) + c)
    pb = ((1 - c) * (1 - y) + c * y, 2 * ((1 - c) * x + c * (1 - x)) + c)
    chip = y * 2 + x
    chip_a = pa[0] * 2 + pa[1] // 2
    chip_b = pb[0] * 2 + pb[1] // 2
    chip_d = (1 - y) * 2 + 1 - x
    sibling = peers[3]

    def remote(src, dst, ss, rs, dev):
        return pltpu.make_async_remote_copy(src_ref=src, dst_ref=dst, send_sem=ss, recv_sem=rs,
                                            device_id=dev, device_id_type=MESH)

    def urows(k, dev):
        return ug.at[k, pl.ds(pl.multiple_of(dev * b, b), b)]

    def ag(k, j):
        return remote(u_ref.at[:, pl.ds(k * kc, kc)], urows(k, me), ag_s.at[k, j], ag_r.at[k, j], peers[j])

    def fw(k, j):
        src = peers[j][0] * nx + peers[j][1]
        return remote(urows(k, src), urows(k, src), fw_s.at[k, j], fw_r.at[k, j], sibling)

    def rts(i):
        t = lax.rem(me + i, 8)
        return remote(rt_ref, rt.at[me], rt_s.at[i - 1], rt_r.at[i - 1], (t // nx, lax.rem(t, nx)))

    def copy_a(t, k, e):
        slot = t % NA if isinstance(t, int) else lax.rem(t, NA)
        ks = pl.ds(k * kc if isinstance(k, int) else pl.multiple_of(k * kc, kc), kc)
        s1 = ws1.at[ks] if e is None else w1.at[e, ks]
        s3 = ws3.at[ks] if e is None else w3.at[e, ks]
        return (pltpu.make_async_copy(s1, ring_a.at[slot, :, pl.ds(0, f)], a_sem.at[slot, 0]),
                pltpu.make_async_copy(s3, ring_a.at[slot, :, pl.ds(f, f)], a_sem.at[slot, 1]))

    def copy_b(t, n, e):
        slot = t % NB if isinstance(t, int) else lax.rem(t, NB)
        ns = pl.ds(n * NC if isinstance(n, int) else pl.multiple_of(n * NC, NC), NC)
        src = ws2.at[:, ns] if e is None else w2.at[e, :, ns]
        return pltpu.make_async_copy(src, ring_b.at[slot], b_sem.at[slot])

    def start_a(t):
        for q in (copy_a(t, t, None) if t < nk else copy_a(t, (t - nk) // edev, (t - nk) % edev)):
            q.start()

    def start_b(t):
        (copy_b(t, t, None) if t < nn else copy_b(t, (t - nn) // edev, (t - nn) % edev)).start()

    for t in range(NA):
        start_a(t)
    for t in range(NB):
        start_b(t)
    own = [pltpu.make_async_copy(u_ref.at[:, pl.ds(k * kc, kc)], urows(k, me), loc_sem.at[k]) for k in range(nk)]
    for q in own:
        q.start()
    own_h = pltpu.make_async_copy(h_ref, hv, loc_sem.at[nk])
    own_h.start()
    own_rt = pltpu.make_async_copy(rt_ref, rt.at[me], loc_sem.at[nk + 1])
    own_rt.start()

    barrier = pltpu.get_barrier_semaphore()
    for i in range(1, 8):
        t = lax.rem(me + i, 8)
        pl.semaphore_signal(barrier, inc=1, device_id=(t // nx, lax.rem(t, nx)), device_id_type=MESH)
    pl.semaphore_wait(barrier, 7)

    for i in range(1, 8):
        rts(i).start()
    for k in range(nk):
        for j in range(4):
            ag(k, j).start()

    for q in own:
        q.wait()
    for t in range(nk):
        for q in copy_a(t, t, None):
            q.wait()
        r = jnp.dot(ug[t, pl.ds(pl.multiple_of(me * b, b), b), :], ring_a[t % NA], preferred_element_type=F32)
        if t == 0:
            acc_s[...] = r
        else:
            acc_s[...] += r
        start_a(t + NA)

    def swiglu(g, v):
        return (g * (1.0 / (1.0 + jnp.exp(-g))) * v).astype(BF)

    z_s[...] = swiglu(acc_s[:, :f], acc_s[:, f:])

    own_rt.wait()
    for i in range(1, 8):
        rts(i).wait_recv()
    for s in range(8):
        tk = rt[s, 0:8, :]
        gt = rt[s, 8:16, :]
        for e in range(edev):
            m = tk == (me * edev + e).astype(F32)
            keys[s * edev + e:s * edev + e + 1, :] = jnp.sum(jnp.where(m, 1.0, 0.0), axis=0, keepdims=True)
            gts[s * edev + e:s * edev + e + 1, :] = jnp.sum(jnp.where(m, gt, 0.0), axis=0, keepdims=True)
    chosen = keys[...]
    before = (lax.broadcasted_iota(jnp.int32, (b, b), 0) < lax.broadcasted_iota(jnp.int32, (b, b), 1))
    rank = jnp.dot(chosen.astype(BF), jnp.where(before, 1.0, 0.0).astype(BF), preferred_element_type=F32)
    keys[...] = jnp.where(chosen > 0.0, rank, -1.0)
    slot_no = lax.broadcasted_iota(jnp.int32, (cap, b), 0).astype(F32)
    zero = jnp.zeros((cap, b), F32)
    for p in range(4):
        parts = []
        for e in range(edev):
            i0, i1 = 2 * p * edev + e, (2 * p + 1) * edev + e
            one0 = jnp.where(keys[i0:i0 + 1, :] == slot_no, 1.0, 0.0)
            one1 = jnp.where(keys[i1:i1 + 1, :] == slot_no, 1.0, 0.0)
            s1h[p, e * half:(e + 1) * half, :] = jnp.concatenate(
                [jnp.concatenate([one0, zero], axis=1), jnp.concatenate([zero, one1], axis=1)], axis=0).astype(BF)
            parts.append(jnp.concatenate(
                [jnp.concatenate([one0 * gts[i0:i0 + 1, :], zero], axis=1),
                 jnp.concatenate([zero, one1 * gts[i1:i1 + 1, :]], axis=1)], axis=0))
        g = jnp.concatenate(parts, axis=0).T
        hi = g.astype(BF)
        rest = g - hi.astype(F32)
        mid = rest.astype(BF)
        lo = (rest - mid.astype(F32)).astype(BF)
        pg[p, 0:2 * b, :] = hi
        pg[p, 2 * b:4 * b, :] = mid
        pg[p, 4 * b:6 * b, :] = lo

    own_h.wait()
    for n in range(nn):
        copy_b(n, n, None).wait()
        sh = jnp.dot(z_s[...], ring_b[n % NB], preferred_element_type=F32).astype(BF).astype(F32)
        base[n] = hv[:, n * NC:(n + 1) * NC].astype(F32) + sh
        start_b(n + NB)

    def forward(k):
        for j in range(3):
            ag(k, j).wait_recv()
            fw(k, j).start()

    forward(0)
    for k in range(nk):
        ag(k, 3).wait_recv()
        for j in range(3):
            fw(k, j).wait_recv()
        for p in range(4):
            dsp = jnp.dot(s1h[p], ug[k, p * 2 * b:(p + 1) * 2 * b, :], preferred_element_type=F32).astype(BF)
            for e in range(edev):
                xin[e, p * half:(p + 1) * half, :] = dsp[e * half:(e + 1) * half]

        def expert(e, carry, k=k):
            i = k * edev + e
            t = i + nk
            slot = lax.rem(t, NA)
            for q in copy_a(t, k, e):
                q.wait()
            rs = pl.ds(pl.multiple_of(e * rows, rows), rows)
            r = jnp.dot(xin[e], ring_a[slot], preferred_element_type=F32)
            if k == 0:
                acc[rs, :] = r
            else:
                acc[rs, :] += r

            @pl.when(i + NA < nk * edev)
            def _():
                i2 = i + NA
                for q in copy_a(t + NA, i2 // edev, lax.rem(i2, edev)):
                    q.start()
            if k == nk - 1:
                z[e] = swiglu(acc[rs, pl.ds(0, f)], acc[rs, pl.ds(f, f)])
            return carry
        if k + 1 < nk:
            lax.fori_loop(0, edev - 2, expert, 0)
            forward(k + 1)
            lax.fori_loop(edev - 2, edev, expert, 0)
        else:
            lax.fori_loop(0, edev, expert, 0)

    def part(n, core, p):
        col = (core * 4 + p) * NC
        col = col if isinstance(col, int) else pl.multiple_of(col, NC)
        return (pl.ds(pl.multiple_of(n * b, b), b), pl.ds(col, NC))

    def to_sib(n):
        src = acc.at[pl.ds(pl.multiple_of(n * b, b), b), pl.ds(pl.multiple_of((1 - c) * 4 * NC, 4 * NC), 4 * NC)]
        return remote(src, sib.at[n], sb_s.at[n], sb_r.at[n], sibling)

    def send_d(n):
        return remote(acc.at[part(n, c, chip_d)], r_d.at[n], rd_s.at[n], rd_r.at[n], pa)

    def send_a(n):
        return remote(acc.at[part(n, c, chip_a)], r_a.at[n], ra_s.at[n], ra_r.at[n], pa)

    def send_b(n):
        return remote(acc.at[part(n, c, chip_b)], r_b.at[n], rb_s.at[n], rb_r.at[n], pb)

    def both(n, p):
        return acc[part(n, c, p)] + sib[n, :, pl.ds(pl.multiple_of(p * NC, NC), NC)]

    def stage1(n):
        to_sib(n).wait_recv()
        acc[part(n, c, chip_d)] = both(n, chip_d)
        send_d(n).start()
        acc[part(n, c, chip_a)] = both(n, chip_a)
        send_a(n).start()
        base[n] += both(n, chip)

    def stage2(n):
        send_d(n).wait_recv()
        acc[part(n, c, chip_b)] = both(n, chip_b) + r_d[n]
        send_b(n).start()

    def block(n, carry):
        def down(e, cc):
            i = n * edev + e
            t = i + nn
            slot = lax.rem(t, NB)
            copy_b(t, n, e).wait()
            r = jnp.dot(z[e], ring_b[slot], preferred_element_type=F32).astype(BF)
            for p in range(4):
                fb[p, pl.ds(pl.multiple_of(e * half, half), half), :] = r[p * half:(p + 1) * half]

            @pl.when(i + NB < nn * edev)
            def _():
                i2 = i + NB
                copy_b(t + NB, i2 // edev, lax.rem(i2, edev)).start()
            return cc
        lax.fori_loop(0, edev // 2, down, 0)

        @pl.when(n > 0)
        def _():
            stage1(n - 1)
        lax.fori_loop(edev // 2, edev, down, 0)
        for p in range(4):
            q = jnp.dot(pg[p], fb[p], preferred_element_type=F32)
            q = q[0:2 * b] + q[2 * b:4 * b] + q[4 * b:6 * b]
            for core in range(2):
                acc[part(n, core, p)] = q[core * b:(core + 1) * b]
        to_sib(n).start()

        @pl.when(n > 0)
        def _():
            stage2(n - 1)
        return carry
    lax.fori_loop(0, nn, block, 0)
    stage1(nn - 1)
    stage2(nn - 1)
    for n in range(nn):
        send_a(n).wait_recv()
        send_b(n).wait_recv()
        y_ref[:, n * NC:(n + 1) * NC] = (base[n] + r_a[n] + r_b[n]).astype(BF)
    for i in range(1, 8):
        rts(i).wait_send()
    for k in range(nk):
        for j in range(4):
            ag(k, j).wait_send()
        for j in range(3):
            fw(k, j).wait_send()
    for n in range(nn):
        to_sib(n).wait_send()
        send_d(n).wait_send()
        send_a(n).wait_send()
        send_b(n).wait_send()


def _moe(u, h, rt, ws1, ws3, ws2, w1, w3, w2, ny, nx):
    b, d = u.shape
    edev, _, f = w1.shape
    cap = 24
    kc, nk, nn = 512, d // 512, d // NC
    dims = (b, d, f, edev, cap, ny, nx, kc, nk, nn)
    dma = pltpu.SemaphoreType.DMA
    anys = pl.BlockSpec(memory_space=pl.ANY)
    return pl.pallas_call(
        functools.partial(_moe_kernel, dims),
        out_shape=jax.ShapeDtypeStruct((b, d), BF),
        in_specs=[anys] * 9,
        out_specs=pl.BlockSpec(memory_space=pltpu.VMEM),
        scratch_shapes=[
            pltpu.VMEM((nk, 8 * b, kc), BF),
            pltpu.VMEM((8, 16, b), F32),
            pltpu.VMEM((edev * 8 * cap, 2 * f), F32),
            pltpu.VMEM((edev, 8 * cap, f), BF),
            pltpu.VMEM((edev, 8 * cap, kc), BF),
            pltpu.VMEM((4, edev * 2 * cap, 2 * b), BF),
            pltpu.VMEM((4, 6 * b, edev * 2 * cap), BF),
            pltpu.VMEM((NA, kc, 2 * f), BF),
            pltpu.VMEM((NB, f, NC), BF),
            pltpu.VMEM((4, edev * 2 * cap, NC), BF),
            pltpu.VMEM((b, 2 * f), F32),
            pltpu.VMEM((b, f), BF),
            pltpu.VMEM((nn, b, NC), F32),
            pltpu.VMEM((b, d), BF),
            pltpu.VMEM((nn, b, 4 * NC), F32),
            pltpu.VMEM((nn, b, NC), F32),
            pltpu.VMEM((nn, b, NC), F32),
            pltpu.VMEM((nn, b, NC), F32),
            pltpu.VMEM((8 * edev, b), F32),
            pltpu.VMEM((8 * edev, b), F32),
            dma((nk + 2,)), dma((NA, 2)), dma((NB,)),
            dma((nk, 4)), dma((nk, 4)), dma((nk, 3)), dma((nk, 3)), dma((7,)), dma((7,)),
            dma((nn,)), dma((nn,)), dma((nn,)), dma((nn,)), dma((nn,)), dma((nn,)), dma((nn,)), dma((nn,)),
        ],
        compiler_params=pltpu.CompilerParams(collective_id=0, has_side_effects=True, vmem_limit_bytes=67043328),
        name='moe',
    )(u, h, rt, ws1, ws3, ws2, w1, w3, w2)


def solution(mesh):
    ey, ex = mesh.shape['ey'], mesh.shape['ex']
    rows = P(('ey', 'ex'))
    rep = P()

    def local(x, kv_k, kv_v, lens, topk_idx, gates, ln1, ln2, wq, wo, ws1, ws3, ws2, w1, w3, w2):
        h = _attn(x, kv_k, kv_v, lens, ln1, wq, wo)
        u = _rms(h, ln2)
        pad = ((0, 2), (0, 0))
        rt = jnp.concatenate([jnp.pad(topk_idx.astype(F32).T, pad, constant_values=-1.0), jnp.pad(gates.T, pad)])
        return _moe(u, h, rt, ws1, ws3, ws2, w1, w3, w2, ey, ex)

    return jax.shard_map(
        local, mesh=mesh,
        in_specs=(rows, rows, rows, rows, rows, rows, rep, rep, rep, rep, rep, rep, rep, rows, rows, rows),
        out_specs=rows, check_vma=False)
```

time: 369 us -> 135 us (0.37)
  Pallas kernels: 0 us -> 96.4 us
  waiting for transfers between devices: 85.4 us -> 0 us
  blocking collectives: 84.4 us -> 0 us
  matrix products: 103 us -> 26.1 us
  local copies, waits for them, and re-layouts: 44.9 us -> 2.8 us
  other arithmetic: 32 us -> 9.03 us
  between operations: 13.8 us -> 0.17 us
  starting transfers between devices: 5.41 us -> 0 us
    pallas_call x0 -> x1, Pallas kernels: none -> 96.4 us  [_moe(): pl.pallas_call(functools.partial(_moe_kernel, dims), out_shape=jax.ShapeD...]
    dot_general x5 -> x0, matrix products: 77 us -> none  [the longest x1 25.2 us: _experts(): v = jnp.einsum('erd,edf->erf', xin, w3, preferred_element_type=F32)]
    all_to_all x1 -> x0, blocking collectives: 74.3 us -> none  [local(): recv = lax.all_to_all(send, 'ex', 0, 0)]
    all_to_all x1 -> x0, waiting for transfers between devices: 59.3 us -> none  [local(): ret = lax.all_to_all(back, 'ex', 0, 0).reshape(nslotv, d)]
    reduce_scatter x1 -> x0, waiting for transfers between devices: 26.1 us -> none  [local(): lax.psum_scatter(partial[:ey * b].reshape(ey, b, d), 'ey', scatter_dimens...]
    scatter-add x1 -> x0, other arithmetic: 23 us -> none  [local(): jnp.zeros((ey * b + 1, d), F32).at[slot_tok]]
    gather x4 -> x0, local copies, waits for them, and re-layouts: 20 us -> none  [the longest x3 12.9 us: _ranks(): return jnp.take_along_axis(before, topk, axis=-1)]
    scatter x2 -> x0, local copies, waits for them, and re-layouts: 12.8 us -> none  [the longest x1 6.4 us: local(): jnp.zeros((nslotv,), F32).at[pos].set(g_g.reshape(-1), mode='drop')]
  transfers between devices with their start and end apart: 3 -> 0, of which waited for: 2 -> 0; matrix products, arithmetic and copies ran while one was open for 8% -> 0% of each run, Pallas kernels for 0% -> 0%
where the time goes in v1:
time: 135 us
  Pallas kernels  96.4 us (71%)
  matrix products  26.1 us (19%)
  other arithmetic  9.03 us (7%)
  local copies, waits for them, and re-layouts  2.8 us (2%)
    pallas_call x1, Pallas kernels, _moe(): pl.pallas_call(functools.partial(_moe_kernel, dims), out_shape=jax.ShapeD...  96.4 us
    dot_general x1, matrix products, _attn(): jnp.einsum('bkgd,blkd->bkgl', q, kk, preferred_element_type=F32)  12.2 us
    dot_general x1, matrix products, _attn(): jnp.einsum('bkgl,blkd->bkgd', p, vv, preferred_element_type=F32).astype(BF)  7.53 us
    sub x1, other arithmetic, _attn(): p = jax.nn.softmax(s, axis=-1).astype(BF)  5.41 us
    dot_general x1, matrix products, _attn(): jnp.dot(a, wq, preferred_element_type=F32).astype(BF)  4.89 us
    unnamed x18, local copies, waits for them, and re-layouts  2.8 us

profile of v1, /device:TPU:0, one launch (start us, length us, event | category | flops | bytes accessed | tf_op | source)
XLA Modules:
  0.0 134.6 jit_solution(454824104774096298)
XLA Ops:
  0.0 0.7 convert_element_type.39
  0.7 1.2 fusion.18
  1.9 4.9 %fusion.14 = bf16[16,8,16,128]{3,1,2,0:T(8,128)(2,1)S(1)} fusion(bf16[2048,2048]{1,0:T(8,128)(2,1)} %param.24, bf16[128,2048]{1,0:T(8,128)(2,1)} %param.16, f32[2048]{0:T(1024)S(1)} %convert_element_type.39, f32[128]{0:T(128)S(1)} %add_rsqrt_fusion.1), kind=kOutput, calls=%fused_computation.21 | convolution fusion | flops 1075052544 | bytes 9445888 | tf_op jit(solution)/shard_map/dot_general | solution.py:30
  6.8 0.1 copy.17
  7.0 0.0 copy-start.5
  7.0 12.2 %fusion.3 = f32[128,16,512]{2,1,0:T(8,128)} fusion(bf16[128,16,128]{2,1,0:T(8,128)(2,1)S(1)} %bitcast.25, bf16[128,512,1,128]{3,1,2,0:T(8,128)(2,1)} %param.17), kind=kOutput, calls=%fused_computation.3 | convolution fusion | flops 268435456 | bytes 21495808 | tf_op jit(solution)/shard_map/bkgd,blkd->bkgl/dot_general | solution.py:31
  19.2 0.1 iota_compare_fusion
  19.3 0.0 slice-start
  19.3 5.4 %fusion.28 = (f32[128,16]{1,0:T(8,128)S(1)}, f32[128,16,512]{2,1,0:T(8,128)S(1)}) fusion(f32[128,16,512]{2,1,0:T(8,128)} %fusion.3, pred[128,512]{1,0:T(8,128)(4,1)S(1)} %iota_compare_fusion), kind=kOutput, calls=%fused_computation.41 | output fusion | flops 6291967 | bytes 8462336 | tf_op jit(solution)/shard_map/sub | solution.py:34
  24.7 0.0 slice-start.1
  24.7 0.0 copy-start
  24.7 7.5 %fusion.11 = bf16[128,16,128]{2,1,0:T(8,128)(2,1)S(1)} fusion(bf16[128,512,1,128]{3,1,2,0:T(8,128)(2,1)} %param.18, f32[128,16,512]{2,1,0:T(8,128)S(1)} %get-tuple-element.6, f32[128,16]{1,0:T(8,128)S(1)} %get-tuple-element.5), kind=kOutput, calls=%fused_computation.20 | convolution fusion | flops 270794752 | bytes 21504000 | tf_op jit(solution)/shard_map/bkgl,blkd->bkgd/dot_general | solution.py:35
  32.3 0.0 slice-done
  32.3 0.0 slice-done.1
  32.3 0.0 copy-done
  32.3 0.0 copy-start.2
  32.3 0.0 copy-start.3
  32.3 0.0 copy-start.4
  32.3 1.5 %fusion.15 = (f32[128]{0:T(128)S(1)}, bf16[128,2048]{1,0:T(8,128)(2,1)S(1)}) fusion(bf16[2048,2048]{1,0:T(8,128)(2,1)S(1)} %bitcast.24, bf16[16,8,16,128]{3,2,1,0:T(8,128)(2,1)S(1)} %bitcast.26, bf16[128,2048]{1,0:T(8,128)(2,1)S(1)} %copy-done), kind=kOutput, calls=%fused_computation.22 | convolution fusion | flops 1075314560 | bytes 9961984 | tf_op jit(solution)/shard_map/dot_general | solution.py:36
  33.9 0.8 copy-done.1
  34.6 1.0 fusion.17.u_ref
  35.6 0.6 select_maximum_fusion.rt_ref
  36.2 96.4 %moe.1 = bf16[128,2048]{1,0:T(8,128)(2,1)} custom-call(bf16[128,2048]{1,0:T(8,128)(2,1)} %fusion.17.u_ref, bf16[128,2048]{1,0:T(8,128)(2,1)} %copy-done.1, f32[16,128]{1,0:T(8,128)} %select_maximum_fusion.rt_ref, bf16[2048,1408]{1,0:T(8,128)(2,1)} %ws1.1, bf16[2048,1408]{1,0:T(8,128)(2,1)} %ws3.1, bf16[1408,2048]{1,0:T(8,128)(2,1)} %ws2.1, ...), custom_call_target="tpu_custom_call" | custom-call | tf_op jit(solution)/shard_map/moe/pallas_call | solution.py:322
  132.7 1.9 %copy.26 = bf16[128,2048]{1,0:T(8,128)(2,1)} copy(bf16[128,2048]{1,0:T(8,128)(2,1)} %moe.1) | data formatting | bytes 1048576
  (10 shorter events, 0.0 us)
Async XLA Ops:
  7.0 12.2 %copy-start.5 = (s32[128]{0:T(128)S(1)}, s32[128]{0:T(128)}, u32[]{:S(2)}) copy-start(s32[128]{0:T(128)} %param.19) | copy-start | bytes 1540
  19.3 13.0 %slice-start = ((s8[8388608]{0:T(1024)(128)(4,1)}), s8[4194304]{0:T(1024)(128)(4,1)S(1)}, s32[]{:S(2)}) async-start(s8[8388608]{0:T(1024)(128)(4,1)} %bitcast.23), calls=%async_computation | async-start | bytes 8388608
  24.7 7.6 %slice-start.1 = ((s8[8388608]{0:T(1024)(128)(4,1)}), s8[4194304]{0:T(1024)(128)(4,1)S(1)}, s32[]{:S(2)}) async-start(s8[8388608]{0:T(1024)(128)(4,1)} %bitcast.23), calls=%async_computation.1 | async-start | bytes 8388608
  24.7 7.6 %copy-start = (bf16[128,2048]{1,0:T(8,128)(2,1)S(1)}, bf16[128,2048]{1,0:T(8,128)(2,1)}, u32[]{:S(2)}) copy-start(bf16[128,2048]{1,0:T(8,128)(2,1)} %param.16) | copy-start | bytes 1572868
  32.3 1.6 %copy-start.2 = (bf16[2048]{0:T(1024)(128)(2,1)S(1)}, bf16[2048]{0:T(1024)(128)(2,1)}, u32[]{:S(2)}) copy-start(bf16[2048]{0:T(1024)(128)(2,1)} %param.23) | copy-start | bytes 12292
  32.3 3.3 %copy-start.3 = (s32[128,6]{0,1:T(8,128)S(1)}, s32[128,6]{0,1:T(8,128)}, u32[]{:S(2)}) copy-start(s32[128,6]{0,1:T(8,128)} %param.20) | copy-start | bytes 9220
  32.3 3.3 %copy-start.4 = (f32[128,6]{0,1:T(8,128)S(1)}, f32[128,6]{0,1:T(8,128)}, u32[]{:S(2)}) copy-start(f32[128,6]{0,1:T(8,128)} %param.21) | copy-start | bytes 9220
  33.8 0.8 copy-start.1

commit v2 on v1

--- a/solution.py
+++ b/solution.py
@@ -15,26 +15,184 @@
 NA = 3
 NB = 5
 NC = 256
-
-
-def _rms(v, w):
-    v = v.astype(F32)
-    r = lax.rsqrt(jnp.mean(v * v, axis=-1, keepdims=True) + EPS)
-    return (v * r * w.astype(F32)).astype(BF)
-
-
-def _attn(x, kk, vv, lens, ln1, wq, wo):
-    b, l, kvh, dh = kk.shape
+UP = 8
+UL = 8
+
+
+def _attn_kernel(dims, lens, x_hbm, ln1, ln2, kk, vv, wq, wo, h_ref, u_ref,
+                 kb, vb, wb, q2, o2, xa, xv, shorts, longs, x_sem, k_sem, v_sem, w_sem):
+    b, l, dh, hq, d = dims
+    sh = 64
+    blk = 2 * sh
+    cq = d // 4
+    top = b * l
+
+    xcopy = pltpu.make_async_copy(x_hbm, xv, x_sem)
+    xcopy.start()
+
+    def wcopy(w, i, s):
+        return pltpu.make_async_copy(w.at[:, pl.ds(i * cq, cq)], wb.at[:, pl.ds(i * cq, cq)], w_sem.at[s, i])
+
+    for i in range(4):
+        wcopy(wq, i, 0).start()
+
+    def srow(i):
+        return pl.multiple_of(top - (i // 2 + 1) * blk + lax.rem(i, 2) * sh, sh)
+
+    def kv_s(src, dst, sem, t, i):
+        return pltpu.make_async_copy(src.at[t, pl.ds(0, sh)], dst.at[pl.ds(srow(i), sh)], sem.at[0])
+
+    def kv_l(src, dst, sem, t, i):
+        return pltpu.make_async_copy(src.at[t], dst.at[pl.ds(pl.multiple_of(i * l, l), l)], sem.at[1])
+
+    def sort_rows(t, c):
+        cs, cl = c
+        short = lens[t] <= sh
+        shorts[cs] = t
+        longs[cl] = t
+
+        @pl.when(short)
+        def _():
+            kv_s(kk, kb, k_sem, t, cs).start()
+
+        @pl.when(jnp.logical_not(short))
+        def _():
+            kv_l(kk, kb, k_sem, t, cl).start()
+        one = short.astype(jnp.int32)
+        return cs + one, cl + 1 - one
+    ns, nl = lax.fori_loop(0, b, sort_rows, (0, 0))
+    odd = lax.rem(ns, 2)
+
+    @pl.when(odd == 1)
+    def _():
+        kv_s(kk, kb, k_sem, shorts[ns - 1], ns).start()
+    last = shorts[jnp.maximum(ns - 1, 0)]
+    for j in range(2 * UP):
+        shorts[ns + j] = last
+    last = longs[jnp.maximum(nl - 1, 0)]
+    for j in range(UL):
+        longs[nl + j] = last
+    ns2 = ns + odd
+
+    def issue_s(i, c):
+        kv_s(vv, vb, v_sem, shorts[i], i).start()
+        return c
+    lax.fori_loop(0, ns2, issue_s, 0)
+
+    def issue_l(i, c):
+        kv_l(vv, vb, v_sem, longs[i], i).start()
+        return c
+    lax.fori_loop(0, nl, issue_l, 0)
+
+    xcopy.wait()
+    x = xv[...].astype(F32)
+    r = lax.rsqrt(jnp.mean(x * x, axis=-1, keepdims=True) + EPS)
+    xa[...] = (x * r * ln1[...].astype(F32)).astype(BF)
+    for j in range(4):
+        wcopy(wq, j, 0).wait()
+        q = jnp.dot(xa[...], wb[:, j * cq:(j + 1) * cq], preferred_element_type=F32)
+        for hh in range(cq // dh):
+            q2[pl.ds(j * (cq // dh) + hh, b, stride=hq), :] = q[:, hh * dh:(hh + 1) * dh].astype(BF).astype(F32)
+        wcopy(wo, j, 1).start()
+
+    def wait_s(i, c):
+        kv_s(kk, kb, k_sem, 0, 0).wait()
+        kv_s(vv, vb, v_sem, 0, 0).wait()
+        return c
+    lax.fori_loop(0, ns2, wait_s, 0)
+
+    def wait_l(i, c):
+        kv_l(kk, kb, k_sem, 0, 0).wait()
+        kv_l(vv, vb, v_sem, 0, 0).wait()
+        return c
+    lax.fori_loop(0, nl, wait_l, 0)
+
+    def qrows(t):
+        return pl.ds(pl.multiple_of(t * hq, hq), hq)
+
+    def normal(s):
+        e = jnp.exp(s - jnp.max(s, axis=-1, keepdims=True))
+        return (e * (1.0 / jnp.sum(e, axis=-1, keepdims=True))).astype(BF)
+
+    nt = (((1,), (1,)), ((), ()))
+    pos2 = lax.broadcasted_iota(jnp.int32, (hq, blk), 1)
+    scale = dh ** -0.5
+
+    def pairs(it, c):
+        ss, idx = [], []
+        for j in range(UP):
+            i = jnp.minimum(it * UP + j, (ns2 // 2) - 1)
+            t0, t1 = shorts[2 * i], shorts[2 * i + 1]
+            q = jnp.concatenate([q2[qrows(t0), :], q2[qrows(t1), :]], axis=0).astype(BF)
+            kr = pl.ds(pl.multiple_of(top - (i + 1) * blk, blk), blk)
+            ss.append(lax.dot_general(q, kb[kr, :], nt, preferred_element_type=F32) * scale)
+            idx.append((t0, t1, kr))
+        for j in range(UP):
+            t0, t1, kr = idx[j]
+            s0 = jnp.where(pos2 < lens[t0], ss[j][:hq], -jnp.inf)
+            s1 = jnp.where(jnp.logical_and(pos2 >= sh, pos2 < sh + lens[t1]), ss[j][hq:], -jnp.inf)
+            o = jnp.dot(normal(jnp.concatenate([s0, s1], axis=0)), vb[kr, :], preferred_element_type=F32)
+            o2[qrows(t0), :] = o[:hq]
+            o2[qrows(t1), :] = o[hq:]
+        return c
+    lax.fori_loop(0, (ns2 // 2 + UP - 1) // UP, pairs, 0)
+
+    pos = lax.broadcasted_iota(jnp.int32, (hq, l), 1)
+
+    def single(it, c):
+        ss, idx = [], []
+        for j in range(UL):
+            i = jnp.minimum(it * UL + j, nl - 1)
+            t = longs[i]
+            kr = pl.ds(pl.multiple_of(i * l, l), l)
+            ss.append(lax.dot_general(q2[qrows(t), :].astype(BF), kb[kr, :], nt, preferred_element_type=F32) * scale)
+            idx.append((t, kr))
+        for j in range(UL):
+            t, kr = idx[j]
+            p = normal(jnp.where(pos < lens[t], ss[j], -jnp.inf))
+            o2[qrows(t), :] = jnp.dot(p, vb[kr, :], preferred_element_type=F32)
+        return c
+    lax.fori_loop(0, (nl + UL - 1) // UL, single, 0)
+
+    for hh in range(hq):
+        xa[:, hh * dh:(hh + 1) * dh] = o2[pl.ds(hh, b, stride=hq), :].astype(BF)
+    ssq = jnp.zeros((b, 1), F32)
+    for j in range(4):
+        cs = slice(j * cq, (j + 1) * cq)
+        wcopy(wo, j, 1).wait()
+        hv = (xv[:, cs].astype(F32) + jnp.dot(xa[...], wb[:, cs], preferred_element_type=F32)).astype(BF)
+        h_ref[:, cs] = hv
+        hf = hv.astype(F32)
+        ssq += jnp.sum(hf * hf, axis=-1, keepdims=True)
+    r = lax.rsqrt(ssq * (1.0 / d) + EPS)
+    for j in range(4):
+        cs = slice(j * cq, (j + 1) * cq)
+        u_ref[:, cs] = (h_ref[:, cs].astype(F32) * r * ln2[:, cs].astype(F32)).astype(BF)
+
+
+def _attn(x, kk, vv, lens, ln1, ln2, wq, wo):
+    b, d = x.shape
+    l, dh = kk.shape[1], kk.shape[3]
     hq = wq.shape[1] // dh
-    a = _rms(x, ln1)
-    q = jnp.dot(a, wq, preferred_element_type=F32).astype(BF).reshape(b, kvh, hq // kvh, dh)
-    s = jnp.einsum('bkgd,blkd->bkgl', q, kk, preferred_element_type=F32) * dh ** -0.5
-    valid = jnp.arange(l)[None, :] < lens[:, None]
-    s = jnp.where(valid[:, None, None, :], s, -jnp.inf)
-    p = jax.nn.softmax(s, axis=-1).astype(BF)
-    o = jnp.einsum('bkgl,blkd->bkgd', p, vv, preferred_element_type=F32).astype(BF)
-    attn = jnp.dot(o.reshape(b, hq * dh), wo, preferred_element_type=F32)
-    return (x.astype(F32) + attn).astype(BF)
+    kk, vv = kk.reshape(b, l, dh), vv.reshape(b, l, dh)
+    dma = pltpu.SemaphoreType.DMA
+    anys = pl.BlockSpec(memory_space=pl.ANY)
+    vm = pl.BlockSpec(memory_space=pltpu.VMEM)
+    return pl.pallas_call(
+        functools.partial(_attn_kernel, (b, l, dh, hq, d)),
+        out_shape=(jax.ShapeDtypeStruct((b, d), BF), jax.ShapeDtypeStruct((b, d), BF)),
+        in_specs=[pl.BlockSpec(memory_space=pltpu.SMEM), anys, vm, vm, anys, anys, anys, anys],
+        out_specs=(vm, vm),
+        scratch_shapes=[
+            pltpu.VMEM((b * l, dh), BF), pltpu.VMEM((b * l, dh), BF), pltpu.VMEM((d, d), BF),
+            pltpu.VMEM((b * hq, dh), F32), pltpu.VMEM((b * hq, dh), F32),
+            pltpu.VMEM((b, d), BF), pltpu.VMEM((b, d), BF),
+            pltpu.SMEM((b + 2 * UP + 2,), jnp.int32), pltpu.SMEM((b + UL + 2,), jnp.int32),
+            dma, dma((2,)), dma((2,)), dma((2, 4)),
+        ],
+        compiler_params=pltpu.CompilerParams(vmem_limit_bytes=67043328),
+        name='attn',
+    )(lens, x, ln1.reshape(1, d), ln2.reshape(1, d), kk, vv, wq, wo)
 
 
 def _moe_kernel(dims, u_ref, h_ref, rt_ref, ws1, ws3, ws2, w1, w3, w2, y_ref,
@@ -360,8 +518,7 @@
     rep = P()
 
     def local(x, kv_k, kv_v, lens, topk_idx, gates, ln1, ln2, wq, wo, ws1, ws3, ws2, w1, w3, w2):
-        h = _attn(x, kv_k, kv_v, lens, ln1, wq, wo)
-        u = _rms(h, ln2)
+        h, u = _attn(x, kv_k, kv_v, lens, ln1, ln2, wq, wo)
         pad = ((0, 2), (0, 0))
         rt = jnp.concatenate([jnp.pad(topk_idx.astype(F32).T, pad, constant_values=-1.0), jnp.pad(gates.T, pad)])
         return _moe(u, h, rt, ws1, ws3, ws2, w1, w3, w2, ey, ex)

time: 135 us -> 123 us (0.911)
  matrix products: 26.1 us -> 0 us
  Pallas kernels: 96.4 us -> 116 us
  other arithmetic: 9.03 us -> 1.98 us
  local copies, waits for them, and re-layouts: 2.8 us -> 4.45 us
    dot_general x4 -> x0, matrix products: 26.1 us -> none  [the longest x1 12.2 us: _attn(): jnp.einsum('bkgd,blkd->bkgl', q, kk, preferred_element_type=F32)]
    pallas_call x0 -> x1, Pallas kernels: none -> 18.1 us  [_attn(): pl.pallas_call(functools.partial(_attn_kernel, (b, l, dh, hq, d)), out_sh...]
    sub x1 -> x0, other arithmetic: 5.41 us -> none  [_attn(): p = jax.nn.softmax(s, axis=-1).astype(BF)]
    reshape x0 -> x2, local copies, waits for them, and re-layouts: none -> 2.57 us  [the longest x1 1.29 us: _attn(): ln2.reshape(1, d)]
    convert_element_type x3 -> x0, other arithmetic: 1.67 us -> none  [_rms(): return (v * r * w.astype(F32)).astype(BF)]
    pallas_call x1, Pallas kernels: 96.4 us -> 98.1 us  [_moe(): pl.pallas_call(functools.partial(_moe_kernel, dims), out_shape=jax.ShapeD...]
    unnamed x18 -> x1, local copies, waits for them, and re-layouts: 2.8 us -> 1.88 us
where the time goes in v2:
time: 123 us
  Pallas kernels  116 us (94%)
  local copies, waits for them, and re-layouts  4.45 us (4%)
  other arithmetic  1.98 us (2%)
    pallas_call x1, Pallas kernels, _moe(): pl.pallas_call(functools.partial(_moe_kernel, dims), out_shape=jax.ShapeD...  98.1 us
    pallas_call x1, Pallas kernels, _attn(): pl.pallas_call(functools.partial(_attn_kernel, (b, l, dh, hq, d)), out_sh...  18.1 us

profile of v2, /device:TPU:0, one launch (start us, length us, event | category | flops | bytes accessed | tf_op | source)
XLA Modules:
  0.0 122.6 jit_solution(12280989425661779303)
XLA Ops:
  0.0 0.7 convert_bitcast_fusion
  0.7 1.3 %select_maximum_fusion.rt_ref = f32[16,128]{1,0:T(8,128)} fusion(f32[6,128]{1,0:T(8,128)} %bitcast.7, f32[6,128]{1,0:T(8,128)S(1)} %convert_bitcast_fusion), kind=kLoop, calls=%fused_computation | loop fusion | flops 10240 | bytes 14336 | tf_op jit(solution)/shard_map/concatenate | solution.py:523
  2.0 1.3 %reshape.12.ln1 = bf16[1,2048]{1,0:T(2,128)(2,1)} reshape(bf16[2048]{0:T(1024)(128)(2,1)} %param.22) | data formatting | bytes 8192 | tf_op jit(solution)/shard_map/reshape | solution.py:195
  3.3 1.3 %reshape.13.ln2 = bf16[1,2048]{1,0:T(2,128)(2,1)} reshape(bf16[2048]{0:T(1024)(128)(2,1)} %param.23) | data formatting | bytes 8192 | tf_op jit(solution)/shard_map/reshape | solution.py:195
  4.5 18.1 %attn.1 = (bf16[128,2048]{1,0:T(8,128)(2,1)}, bf16[128,2048]{1,0:T(8,128)(2,1)}) custom-call(s32[128]{0:T(128)} %lens.1, bf16[128,2048]{1,0:T(8,128)(2,1)} %x_hbm.1, bf16[1,2048]{1,0:T(2,128)(2,1)} %reshape.12.ln1, bf16[1,2048]{1,0:T(2,128)(2,1)} %reshape.13.ln2, bf16[128,512,128]{2,1,0:T(8,128)(2,1)} %bitcast.5, bf16[128,512,128]{2,1,0:T(8,128)(2,1)} %bitcast.6, ...), custom_call_target="tpu_custom_call" | custom-call | tf_op jit(solution)/shard_map/attn/pallas_call | solution.py:181
  22.7 98.1 %moe.1 = bf16[128,2048]{1,0:T(8,128)(2,1)} custom-call(bf16[128,2048]{1,0:T(8,128)(2,1)} %get-tuple-element.7.u_ref, bf16[128,2048]{1,0:T(8,128)(2,1)} %get-tuple-element.8.h_ref, f32[16,128]{1,0:T(8,128)} %select_maximum_fusion.rt_ref, bf16[2048,1408]{1,0:T(8,128)(2,1)} %ws1.1, bf16[2048,1408]{1,0:T(8,128)(2,1)} %ws3.1, bf16[1408,2048]{1,0:T(8,128)(2,1)} %ws2.1, ...), custom_call_target="tpu_custom_call" | custom-call | tf_op jit(solution)/shard_map/moe/pallas_call | solution.py:480
  120.7 1.9 %copy.18 = bf16[128,2048]{1,0:T(8,128)(2,1)} copy(bf16[128,2048]{1,0:T(8,128)(2,1)} %moe.1) | data formatting | bytes 1048576

commit v3 on v2

--- a/solution.py
+++ b/solution.py
@@ -12,14 +12,14 @@
 F32 = jnp.float32
 MESH = pl.DeviceIdType.MESH
 
-NA = 3
+NA = 4
 NB = 5
 NC = 256
 UP = 8
 UL = 8
 
 
-def _attn_kernel(dims, lens, x_hbm, ln1, ln2, kk, vv, wq, wo, h_ref, u_ref,
+def _attn_kernel(dims, lens, x_hbm, ln1, ln2, topk, gates, kk, vv, wq, wo, h_ref, u_ref, rt_ref,
                  kb, vb, wb, q2, o2, xa, xv, shorts, longs, x_sem, k_sem, v_sem, w_sem):
     b, l, dh, hq, d = dims
     sh = 64
@@ -84,10 +84,13 @@
         return c
     lax.fori_loop(0, nl, issue_l, 0)
 
+    k = topk.shape[0]
+    rt_ref[...] = jnp.concatenate(
+        [topk[...].astype(F32), jnp.full((8 - k, b), -1.0, F32), gates[...], jnp.zeros((8 - k, b), F32)], axis=0)
     xcopy.wait()
     x = xv[...].astype(F32)
     r = lax.rsqrt(jnp.mean(x * x, axis=-1, keepdims=True) + EPS)
-    xa[...] = (x * r * ln1[...].astype(F32)).astype(BF)
+    xa[...] = (x * r * ln1[...].astype(F32).reshape(1, d)).astype(BF)
     for j in range(4):
         wcopy(wq, j, 0).wait()
         q = jnp.dot(xa[...], wb[:, j * cq:(j + 1) * cq], preferred_element_type=F32)
@@ -167,10 +170,10 @@
     r = lax.rsqrt(ssq * (1.0 / d) + EPS)
     for j in range(4):
         cs = slice(j * cq, (j + 1) * cq)
-        u_ref[:, cs] = (h_ref[:, cs].astype(F32) * r * ln2[:, cs].astype(F32)).astype(BF)
-
-
-def _attn(x, kk, vv, lens, ln1, ln2, wq, wo):
+        u_ref[:, cs] = (h_ref[:, cs].astype(F32) * r * ln2[cs].astype(F32).reshape(1, cq)).astype(BF)
+
+
+def _attn(x, kk, vv, lens, ln1, ln2, topk, gates, wq, wo):
     b, d = x.shape
     l, dh = kk.shape[1], kk.shape[3]
     hq = wq.shape[1] // dh
@@ -180,9 +183,10 @@
     vm = pl.BlockSpec(memory_space=pltpu.VMEM)
     return pl.pallas_call(
         functools.partial(_attn_kernel, (b, l, dh, hq, d)),
-        out_shape=(jax.ShapeDtypeStruct((b, d), BF), jax.ShapeDtypeStruct((b, d), BF)),
-        in_specs=[pl.BlockSpec(memory_space=pltpu.SMEM), anys, vm, vm, anys, anys, anys, anys],
-        out_specs=(vm, vm),
+        out_shape=(jax.ShapeDtypeStruct((b, d), BF), jax.ShapeDtypeStruct((b, d), BF),
+                   jax.ShapeDtypeStruct((16, b), F32)),
+        in_specs=[pl.BlockSpec(memory_space=pltpu.SMEM), anys, vm, vm, vm, vm, anys, anys, anys, anys],
+        out_specs=(vm, vm, vm),
         scratch_shapes=[
             pltpu.VMEM((b * l, dh), BF), pltpu.VMEM((b * l, dh), BF), pltpu.VMEM((d, d), BF),
             pltpu.VMEM((b * hq, dh), F32), pltpu.VMEM((b * hq, dh), F32),
@@ -192,14 +196,15 @@
         ],
         compiler_params=pltpu.CompilerParams(vmem_limit_bytes=67043328),
         name='attn',
-    )(lens, x, ln1.reshape(1, d), ln2.reshape(1, d), kk, vv, wq, wo)
+    )(lens, x, ln1, ln2, topk.T, gates.T, kk, vv, wq, wo)
 
 
 def _moe_kernel(dims, u_ref, h_ref, rt_ref, ws1, ws3, ws2, w1, w3, w2, y_ref,
                 ug, rt, acc, z, xin, s1h, pg, ring_a, ring_b, fb, acc_s, z_s, base, hv, sib, r_d, r_a, r_b,
                 keys, gts, loc_sem, a_sem, b_sem, ag_s, ag_r, fw_s, fw_r, rt_s, rt_r, sb_s, sb_r,
                 rd_s, rd_r, ra_s, ra_r, rb_s, rb_r):
-    b, d, f, edev, cap, ny, nx, kc, nk, nn = dims
+    b, d, f, edev, cap, ny, nx, kc, chunks, nn = dims
+    nk = len(chunks)
     rows = 8 * cap
     half = 2 * cap
     y = lax.axis_index('ey')
@@ -221,10 +226,10 @@
                                             device_id=dev, device_id_type=MESH)
 
     def urows(k, dev):
-        return ug.at[k, pl.ds(pl.multiple_of(dev * b, b), b)]
+        return ug.at[pl.ds(pl.multiple_of(dev * b, b), b), pl.ds(*chunks[k])]
 
     def ag(k, j):
-        return remote(u_ref.at[:, pl.ds(k * kc, kc)], urows(k, me), ag_s.at[k, j], ag_r.at[k, j], peers[j])
+        return remote(u_ref.at[:, pl.ds(*chunks[k])], urows(k, me), ag_s.at[k, j], ag_r.at[k, j], peers[j])
 
     def fw(k, j):
         src = peers[j][0] * nx + peers[j][1]
@@ -234,13 +239,16 @@
         t = lax.rem(me + i, 8)
         return remote(rt_ref, rt.at[me], rt_s.at[i - 1], rt_r.at[i - 1], (t // nx, lax.rem(t, nx)))
 
-    def copy_a(t, k, e):
-        slot = t % NA if isinstance(t, int) else lax.rem(t, NA)
-        ks = pl.ds(k * kc if isinstance(k, int) else pl.multiple_of(k * kc, kc), kc)
+    def copy_a(slot, start, size, e):
+        ks = pl.ds(start, size)
         s1 = ws1.at[ks] if e is None else w1.at[e, ks]
         s3 = ws3.at[ks] if e is None else w3.at[e, ks]
-        return (pltpu.make_async_copy(s1, ring_a.at[slot, :, pl.ds(0, f)], a_sem.at[slot, 0]),
-                pltpu.make_async_copy(s3, ring_a.at[slot, :, pl.ds(f, f)], a_sem.at[slot, 1]))
+        return (pltpu.make_async_copy(s1, ring_a.at[slot, pl.ds(0, size), pl.ds(0, f)], a_sem.at[slot, 0]),
+                pltpu.make_async_copy(s3, ring_a.at[slot, pl.ds(0, size), pl.ds(f, f)], a_sem.at[slot, 1]))
+
+    def shared_a(i):
+        start = i * kc if isinstance(i, int) else pl.multiple_of(i * kc, kc)
+        return copy_a(i, start, kc, None)
 
     def copy_b(t, n, e):
         slot = t % NB if isinstance(t, int) else lax.rem(t, NB)
@@ -248,24 +256,17 @@
         src = ws2.at[:, ns] if e is None else w2.at[e, :, ns]
         return pltpu.make_async_copy(src, ring_b.at[slot], b_sem.at[slot])
 
-    def start_a(t):
-        for q in (copy_a(t, t, None) if t < nk else copy_a(t, (t - nk) // edev, (t - nk) % edev)):
+    for t in range(NA):
+        for q in copy_a(t, *chunks[0], t):
             q.start()
-
-    def start_b(t):
-        (copy_b(t, t, None) if t < nn else copy_b(t, (t - nn) // edev, (t - nn) % edev)).start()
-
-    for t in range(NA):
-        start_a(t)
+    own = pltpu.make_async_copy(u_ref, ug.at[pl.ds(pl.multiple_of(me * b, b), b)], loc_sem.at[0])
+    own.start()
+    own_h = pltpu.make_async_copy(h_ref, hv, loc_sem.at[1])
+    own_h.start()
+    own_rt = pltpu.make_async_copy(rt_ref, rt.at[me], loc_sem.at[2])
+    own_rt.start()
     for t in range(NB):
-        start_b(t)
-    own = [pltpu.make_async_copy(u_ref.at[:, pl.ds(k * kc, kc)], urows(k, me), loc_sem.at[k]) for k in range(nk)]
-    for q in own:
-        q.start()
-    own_h = pltpu.make_async_copy(h_ref, hv, loc_sem.at[nk])
-    own_h.start()
-    own_rt = pltpu.make_async_copy(rt_ref, rt.at[me], loc_sem.at[nk + 1])
-    own_rt.start()
+        copy_b(t, 0, t).start()
 
     barrier = pltpu.get_barrier_semaphore()
     for i in range(1, 8):
@@ -279,22 +280,8 @@
         for j in range(4):
             ag(k, j).start()
 
-    for q in own:
-        q.wait()
-    for t in range(nk):
-        for q in copy_a(t, t, None):
-            q.wait()
-        r = jnp.dot(ug[t, pl.ds(pl.multiple_of(me * b, b), b), :], ring_a[t % NA], preferred_element_type=F32)
-        if t == 0:
-            acc_s[...] = r
-        else:
-            acc_s[...] += r
-        start_a(t + NA)
-
     def swiglu(g, v):
         return (g * (1.0 / (1.0 + jnp.exp(-g))) * v).astype(BF)
-
-    z_s[...] = swiglu(acc_s[:, :f], acc_s[:, f:])
 
     own_rt.wait()
     for i in range(1, 8):
@@ -332,55 +319,49 @@
         pg[p, 2 * b:4 * b, :] = mid
         pg[p, 4 * b:6 * b, :] = lo
 
-    own_h.wait()
-    for n in range(nn):
-        copy_b(n, n, None).wait()
-        sh = jnp.dot(z_s[...], ring_b[n % NB], preferred_element_type=F32).astype(BF).astype(F32)
-        base[n] = hv[:, n * NC:(n + 1) * NC].astype(F32) + sh
-        start_b(n + NB)
-
     def forward(k):
         for j in range(3):
             ag(k, j).wait_recv()
             fw(k, j).start()
 
     forward(0)
+    own.wait()
     for k in range(nk):
         ag(k, 3).wait_recv()
         for j in range(3):
             fw(k, j).wait_recv()
+        start, size = chunks[k]
         for p in range(4):
-            dsp = jnp.dot(s1h[p], ug[k, p * 2 * b:(p + 1) * 2 * b, :], preferred_element_type=F32).astype(BF)
+            dsp = jnp.dot(s1h[p], ug[p * 2 * b:(p + 1) * 2 * b, start:start + size],
+                          preferred_element_type=F32).astype(BF)
             for e in range(edev):
-                xin[e, p * half:(p + 1) * half, :] = dsp[e * half:(e + 1) * half]
-
-        def expert(e, carry, k=k):
-            i = k * edev + e
-            t = i + nk
-            slot = lax.rem(t, NA)
-            for q in copy_a(t, k, e):
+                xin[e, p * half:(p + 1) * half, 0:size] = dsp[e * half:(e + 1) * half]
+
+        def expert(e, carry, k=k, start=start, size=size, late=False):
+            slot = lax.rem(e, NA)
+            for q in copy_a(slot, start, size, e):
                 q.wait()
             rs = pl.ds(pl.multiple_of(e * rows, rows), rows)
-            r = jnp.dot(xin[e], ring_a[slot], preferred_element_type=F32)
+            r = jnp.dot(xin[e, :, 0:size], ring_a[slot, 0:size, :], preferred_element_type=F32)
             if k == 0:
                 acc[rs, :] = r
             else:
                 acc[rs, :] += r
-
-            @pl.when(i + NA < nk * edev)
-            def _():
-                i2 = i + NA
-                for q in copy_a(t + NA, i2 // edev, lax.rem(i2, edev)):
-                    q.start()
+            if not late:
+                nxt = copy_a(slot, start, size, e + NA)
+            elif k + 1 < nk:
+                nxt = copy_a(slot, *chunks[k + 1], e + NA - edev)
+            else:
+                nxt = shared_a(slot)
+            for q in nxt:
+                q.start()
             if k == nk - 1:
                 z[e] = swiglu(acc[rs, pl.ds(0, f)], acc[rs, pl.ds(f, f)])
             return carry
+        lax.fori_loop(0, edev - NA, expert, 0)
         if k + 1 < nk:
-            lax.fori_loop(0, edev - 2, expert, 0)
             forward(k + 1)
-            lax.fori_loop(edev - 2, edev, expert, 0)
-        else:
-            lax.fori_loop(0, edev, expert, 0)
+        lax.fori_loop(edev - NA, edev, functools.partial(expert, late=True), 0)
 
     def part(n, core, p):
         col = (core * 4 + p) * NC
@@ -408,8 +389,13 @@
         acc[part(n, c, chip_d)] = both(n, chip_d)
         send_d(n).start()
         acc[part(n, c, chip_a)] = both(n, chip_a)
-        send_a(n).start()
-        base[n] += both(n, chip)
+        if isinstance(n, int):
+            send_a(n - 1).start()
+        else:
+            @pl.when(n > 0)
+            def _():
+                send_a(n - 1).start()
+        base[n] = both(n, chip)
 
     def stage2(n):
         send_d(n).wait_recv()
@@ -419,9 +405,8 @@
     def block(n, carry):
         def down(e, cc):
             i = n * edev + e
-            t = i + nn
-            slot = lax.rem(t, NB)
-            copy_b(t, n, e).wait()
+            slot = lax.rem(i, NB)
+            copy_b(i, n, e).wait()
             r = jnp.dot(z[e], ring_b[slot], preferred_element_type=F32).astype(BF)
             for p in range(4):
                 fb[p, pl.ds(pl.multiple_of(e * half, half), half), :] = r[p * half:(p + 1) * half]
@@ -429,7 +414,11 @@
             @pl.when(i + NB < nn * edev)
             def _():
                 i2 = i + NB
-                copy_b(t + NB, i2 // edev, lax.rem(i2, edev)).start()
+                copy_b(i2, i2 // edev, lax.rem(i2, edev)).start()
+
+            @pl.when(i + NB >= nn * edev)
+            def _():
+                copy_b(i + NB, i + NB - nn * edev, None).start()
             return cc
         lax.fori_loop(0, edev // 2, down, 0)
 
@@ -444,13 +433,34 @@
                 acc[part(n, core, p)] = q[core * b:(core + 1) * b]
         to_sib(n).start()
 
-        @pl.when(n > 0)
+        @pl.when(n > 1)
         def _():
-            stage2(n - 1)
+            stage2(n - 2)
         return carry
     lax.fori_loop(0, nn, block, 0)
     stage1(nn - 1)
+    send_a(nn - 1).start()
+    stage2(nn - 2)
+
+    for i in range(d // kc):
+        for q in shared_a(i):
+            q.wait()
+        r = jnp.dot(ug[pl.ds(pl.multiple_of(me * b, b), b), i * kc:(i + 1) * kc], ring_a[i],
+                    preferred_element_type=F32)
+        if i == 0:
+            acc_s[...] = r
+        else:
+            acc_s[...] += r
+    z_s[...] = swiglu(acc_s[:, :f], acc_s[:, f:])
     stage2(nn - 1)
+    own_h.wait()
+    for n in range(nn):
+        t = nn * edev + n
+        copy_b(t, n, None).wait()
+        sh = jnp.dot(z_s[...], ring_b[t % NB], preferred_element_type=F32).astype(BF).astype(F32)
+        base[n] += hv[:, n * NC:(n + 1) * NC].astype(F32) + sh
+        if n + NB < nn:
+            copy_b(t + NB, n + NB, None).start()
     for n in range(nn):
         send_a(n).wait_recv()
         send_b(n).wait_recv()
@@ -473,8 +483,10 @@
     b, d = u.shape
     edev, _, f = w1.shape
     cap = 24
-    kc, nk, nn = 512, d // 512, d // NC
-    dims = (b, d, f, edev, cap, ny, nx, kc, nk, nn)
+    kc, nn = 512, d // NC
+    chunks = ((0, 256), (256, 256), (512, 512), (1024, 512), (1536, 512))
+    nk = len(chunks)
+    dims = (b, d, f, edev, cap, ny, nx, kc, chunks, nn)
     dma = pltpu.SemaphoreType.DMA
     anys = pl.BlockSpec(memory_space=pl.ANY)
     return pl.pallas_call(
@@ -483,7 +495,7 @@
         in_specs=[anys] * 9,
         out_specs=pl.BlockSpec(memory_space=pltpu.VMEM),
         scratch_shapes=[
-            pltpu.VMEM((nk, 8 * b, kc), BF),
+            pltpu.VMEM((8 * b, d), BF),
             pltpu.VMEM((8, 16, b), F32),
             pltpu.VMEM((edev * 8 * cap, 2 * f), F32),
             pltpu.VMEM((edev, 8 * cap, f), BF),
@@ -503,7 +515,7 @@
             pltpu.VMEM((nn, b, NC), F32),
             pltpu.VMEM((8 * edev, b), F32),
             pltpu.VMEM((8 * edev, b), F32),
-            dma((nk + 2,)), dma((NA, 2)), dma((NB,)),
+            dma((3,)), dma((NA, 2)), dma((NB,)),
             dma((nk, 4)), dma((nk, 4)), dma((nk, 3)), dma((nk, 3)), dma((7,)), dma((7,)),
             dma((nn,)), dma((nn,)), dma((nn,)), dma((nn,)), dma((nn,)), dma((nn,)), dma((nn,)), dma((nn,)),
         ],
@@ -518,9 +530,7 @@
     rep = P()
 
     def local(x, kv_k, kv_v, lens, topk_idx, gates, ln1, ln2, wq, wo, ws1, ws3, ws2, w1, w3, w2):
-        h, u = _attn(x, kv_k, kv_v, lens, ln1, ln2, wq, wo)
-        pad = ((0, 2), (0, 0))
-        rt = jnp.concatenate([jnp.pad(topk_idx.astype(F32).T, pad, constant_values=-1.0), jnp.pad(gates.T, pad)])
+        h, u, rt = _attn(x, kv_k, kv_v, lens, ln1, ln2, topk_idx, gates, wq, wo)
         return _moe(u, h, rt, ws1, ws3, ws2, w1, w3, w2, ey, ex)
 
     return jax.shard_map(

time: 123 us -> 110 us (0.89)
  Pallas kernels: 116 us -> 107 us
  local copies, waits for them, and re-layouts: 4.45 us -> 1.88 us
  other arithmetic: 1.98 us -> 0 us
    pallas_call x1, Pallas kernels: 98.1 us -> 88.5 us  [_moe(): pl.pallas_call(functools.partial(_moe_kernel, dims), out_shape=jax.ShapeD...]
    reshape x2 -> x0, local copies, waits for them, and re-layouts: 2.57 us -> none  [the longest x1 1.29 us: _attn(): ln2.reshape(1, d)]
    concatenate x1 -> x0, other arithmetic: 1.29 us -> none  [local(): jnp.concatenate([jnp.pad(topk_idx.astype(F32).T, pad, constant_values=-1....]
where the time goes in v3:
time: 110 us; the launch traced here: 109 us
  Pallas kernels  107 us (97%)
  local copies, waits for them, and re-layouts  1.88 us (2%)
    pallas_call x1, Pallas kernels, _moe(): pl.pallas_call(functools.partial(_moe_kernel, dims), out_shape=jax.ShapeD...  88.5 us
    pallas_call x1, Pallas kernels, _attn(): pl.pallas_call(functools.partial(_attn_kernel, (b, l, dh, hq, d)), out_sh...  18.9 us

profile of v3, /device:TPU:0, one launch (start us, length us, event | category | flops | bytes accessed | tf_op | source)
XLA Modules:
  0.0 109.4 jit_solution(6599295205460474472)
XLA Ops:
  0.0 18.9 %attn.1 = (bf16[128,2048]{1,0:T(8,128)(2,1)}, bf16[128,2048]{1,0:T(8,128)(2,1)}, f32[16,128]{1,0:T(8,128)}) custom-call(s32[128]{0:T(128)} %lens.1, bf16[128,2048]{1,0:T(8,128)(2,1)} %x_hbm.1, bf16[2048]{0:T(1024)(128)(2,1)} %ln1.1, bf16[2048]{0:T(1024)(128)(2,1)} %ln2.1, s32[6,128]{1,0:T(8,128)} %bitcast.6, f32[6,128]{1,0:T(8,128)} %bitcast.7, ...), custom_call_target="tpu_custom_call" | custom-call | tf_op jit(solution)/shard_map/attn/pallas_call | solution.py:184
  18.9 88.5 %moe.1 = bf16[128,2048]{1,0:T(8,128)(2,1)} custom-call(bf16[128,2048]{1,0:T(8,128)(2,1)} %get-tuple-element.8.u_ref, bf16[128,2048]{1,0:T(8,128)(2,1)} %get-tuple-element.9.h_ref, f32[16,128]{1,0:T(8,128)} %get-tuple-element.10.rt_ref, bf16[2048,1408]{1,0:T(8,128)(2,1)} %ws1.1, bf16[2048,1408]{1,0:T(8,128)(2,1)} %ws3.1, bf16[1408,2048]{1,0:T(8,128)(2,1)} %ws2.1, ...), custom_call_target="tpu_custom_call" | custom-call | tf_op jit(solution)/shard_map/moe/pallas_call | solution.py:492
  107.5 1.9 %copy.18 = bf16[128,2048]{1,0:T(8,128)(2,1)} copy(bf16[128,2048]{1,0:T(8,128)(2,1)} %moe.1) | data formatting | bytes 1048576

commit v4 on v3

--- a/solution.py
+++ b/solution.py
@@ -13,14 +13,15 @@
 MESH = pl.DeviceIdType.MESH
 
 NA = 4
-NB = 5
+NB = 8
+ND = 4
 NC = 256
-UP = 8
-UL = 8
+UP = 24
+UL = 24
 
 
 def _attn_kernel(dims, lens, x_hbm, ln1, ln2, topk, gates, kk, vv, wq, wo, h_ref, u_ref, rt_ref,
-                 kb, vb, wb, q2, o2, xa, xv, shorts, longs, x_sem, k_sem, v_sem, w_sem):
+                 kb, vb, wb, q2, o2, xa, xv, shorts, longs, x_sem, kv_sem, w_sem):
     b, l, dh, hq, d = dims
     sh = 64
     blk = 2 * sh
@@ -39,11 +40,18 @@
     def srow(i):
         return pl.multiple_of(top - (i // 2 + 1) * blk + lax.rem(i, 2) * sh, sh)
 
-    def kv_s(src, dst, sem, t, i):
-        return pltpu.make_async_copy(src.at[t, pl.ds(0, sh)], dst.at[pl.ds(srow(i), sh)], sem.at[0])
-
-    def kv_l(src, dst, sem, t, i):
-        return pltpu.make_async_copy(src.at[t], dst.at[pl.ds(pl.multiple_of(i * l, l), l)], sem.at[1])
+    def kv_s(t, i):
+        for q, (src, dst) in enumerate(((kk, kb), (vv, vb))):
+            pltpu.make_async_copy(src.at[t, pl.ds(0, sh)], dst.at[pl.ds(srow(i), sh)], kv_sem.at[0, q]).start()
+
+    def kv_l(t, i):
+        for q, (src, dst) in enumerate(((kk, kb), (vv, vb))):
+            pltpu.make_async_copy(src.at[t], dst.at[pl.ds(pl.multiple_of(i * l, l), l)], kv_sem.at[1, q]).start()
+
+    def kv_wait(kind, n_rows):
+        r = pl.ds(0, pl.multiple_of(n_rows, sh))
+        for q, buf in enumerate((kb, vb)):
+            pltpu.make_async_copy(buf.at[r], buf.at[r], kv_sem.at[kind, q]).wait()
 
     def sort_rows(t, c):
         cs, cl = c
@@ -53,11 +61,11 @@
 
         @pl.when(short)
         def _():
-            kv_s(kk, kb, k_sem, t, cs).start()
+            kv_s(t, cs)
 
         @pl.when(jnp.logical_not(short))
         def _():
-            kv_l(kk, kb, k_sem, t, cl).start()
+            kv_l(t, cl)
         one = short.astype(jnp.int32)
         return cs + one, cl + 1 - one
     ns, nl = lax.fori_loop(0, b, sort_rows, (0, 0))
@@ -65,24 +73,10 @@
 
     @pl.when(odd == 1)
     def _():
-        kv_s(kk, kb, k_sem, shorts[ns - 1], ns).start()
+        kv_s(shorts[ns - 1], ns)
     last = shorts[jnp.maximum(ns - 1, 0)]
-    for j in range(2 * UP):
-        shorts[ns + j] = last
-    last = longs[jnp.maximum(nl - 1, 0)]
-    for j in range(UL):
-        longs[nl + j] = last
+    shorts[ns] = last
     ns2 = ns + odd
-
-    def issue_s(i, c):
-        kv_s(vv, vb, v_sem, shorts[i], i).start()
-        return c
-    lax.fori_loop(0, ns2, issue_s, 0)
-
-    def issue_l(i, c):
-        kv_l(vv, vb, v_sem, longs[i], i).start()
-        return c
-    lax.fori_loop(0, nl, issue_l, 0)
 
     k = topk.shape[0]
     rt_ref[...] = jnp.concatenate(
@@ -97,18 +91,6 @@
         for hh in range(cq // dh):
             q2[pl.ds(j * (cq // dh) + hh, b, stride=hq), :] = q[:, hh * dh:(hh + 1) * dh].astype(BF).astype(F32)
         wcopy(wo, j, 1).start()
-
-    def wait_s(i, c):
-        kv_s(kk, kb, k_sem, 0, 0).wait()
-        kv_s(vv, vb, v_sem, 0, 0).wait()
-        return c
-    lax.fori_loop(0, ns2, wait_s, 0)
-
-    def wait_l(i, c):
-        kv_l(kk, kb, k_sem, 0, 0).wait()
-        kv_l(vv, vb, v_sem, 0, 0).wait()
-        return c
-    lax.fori_loop(0, nl, wait_l, 0)
 
     def qrows(t):
         return pl.ds(pl.multiple_of(t * hq, hq), hq)
@@ -138,6 +120,7 @@
             o2[qrows(t0), :] = o[:hq]
             o2[qrows(t1), :] = o[hq:]
         return c
+    kv_wait(0, ns2 * sh)
     lax.fori_loop(0, (ns2 // 2 + UP - 1) // UP, pairs, 0)
 
     pos = lax.broadcasted_iota(jnp.int32, (hq, l), 1)
@@ -155,6 +138,7 @@
             p = normal(jnp.where(pos < lens[t], ss[j], -jnp.inf))
             o2[qrows(t), :] = jnp.dot(p, vb[kr, :], preferred_element_type=F32)
         return c
+    kv_wait(1, nl * l)
     lax.fori_loop(0, (nl + UL - 1) // UL, single, 0)
 
     for hh in range(hq):
@@ -191,8 +175,8 @@
             pltpu.VMEM((b * l, dh), BF), pltpu.VMEM((b * l, dh), BF), pltpu.VMEM((d, d), BF),
             pltpu.VMEM((b * hq, dh), F32), pltpu.VMEM((b * hq, dh), F32),
             pltpu.VMEM((b, d), BF), pltpu.VMEM((b, d), BF),
-            pltpu.SMEM((b + 2 * UP + 2,), jnp.int32), pltpu.SMEM((b + UL + 2,), jnp.int32),
-            dma, dma((2,)), dma((2,)), dma((2, 4)),
+            pltpu.SMEM((b + 2,), jnp.int32), pltpu.SMEM((b + 2,), jnp.int32),
+            dma, dma((2, 2)), dma((2, 4)),
         ],
         compiler_params=pltpu.CompilerParams(vmem_limit_bytes=67043328),
         name='attn',
@@ -389,12 +373,7 @@
         acc[part(n, c, chip_d)] = both(n, chip_d)
         send_d(n).start()
         acc[part(n, c, chip_a)] = both(n, chip_a)
-        if isinstance(n, int):
-            send_a(n - 1).start()
-        else:
-            @pl.when(n > 0)
-            def _():
-                send_a(n - 1).start()
+        send_a(n).start()
         base[n] = both(n, chip)
 
     def stage2(n):
@@ -403,29 +382,31 @@
         send_b(n).start()
 
     def block(n, carry):
-        def down(e, cc):
-            i = n * edev + e
-            slot = lax.rem(i, NB)
-            copy_b(i, n, e).wait()
-            r = jnp.dot(z[e], ring_b[slot], preferred_element_type=F32).astype(BF)
-            for p in range(4):
-                fb[p, pl.ds(pl.multiple_of(e * half, half), half), :] = r[p * half:(p + 1) * half]
-
-            @pl.when(i + NB < nn * edev)
-            def _():
-                i2 = i + NB
-                copy_b(i2, i2 // edev, lax.rem(i2, edev)).start()
-
-            @pl.when(i + NB >= nn * edev)
-            def _():
-                copy_b(i + NB, i + NB - nn * edev, None).start()
+        def down(e2, cc):
+            es = [e2 * ND + j for j in range(ND)]
+            for e in es:
+                copy_b(n * edev + e, n, e).wait()
+            rs = [jnp.dot(z[e], ring_b[lax.rem(n * edev + e, NB)], preferred_element_type=F32).astype(BF) for e in es]
+            for e, r in zip(es, rs):
+                for p in range(4):
+                    fb[p, pl.ds(pl.multiple_of(e * half, half), half), :] = r[p * half:(p + 1) * half]
+            for e in es:
+                i2 = n * edev + e + NB
+
+                @pl.when(i2 < nn * edev)
+                def _():
+                    copy_b(i2, i2 // edev, lax.rem(i2, edev)).start()
+
+                @pl.when(i2 >= nn * edev)
+                def _():
+                    copy_b(i2, i2 - nn * edev, None).start()
             return cc
-        lax.fori_loop(0, edev // 2, down, 0)
+        lax.fori_loop(0, edev // 2 // ND, down, 0)
 
         @pl.when(n > 0)
         def _():
             stage1(n - 1)
-        lax.fori_loop(edev // 2, edev, down, 0)
+        lax.fori_loop(edev // 2 // ND, edev // ND, down, 0)
         for p in range(4):
             q = jnp.dot(pg[p], fb[p], preferred_element_type=F32)
             q = q[0:2 * b] + q[2 * b:4 * b] + q[4 * b:6 * b]
@@ -436,10 +417,13 @@
         @pl.when(n > 1)
         def _():
             stage2(n - 2)
+
+        @pl.when(n == nn // 2)
+        def _():
+            pass
         return carry
     lax.fori_loop(0, nn, block, 0)
     stage1(nn - 1)
-    send_a(nn - 1).start()
     stage2(nn - 2)
 
     for i in range(d // kc):

time: 110 us -> 107 us (0.973)
  Pallas kernels: 107 us -> 105 us
    pallas_call x1, Pallas kernels: 18.9 us -> 16 us  [_attn(): pl.pallas_call(functools.partial(_attn_kernel, (b, l, dh, hq, d)), out_sh...]
where the time goes in v4:
time: 107 us
  Pallas kernels  105 us (98%)
  local copies, waits for them, and re-layouts  1.88 us (2%)
    pallas_call x1, Pallas kernels, _moe(): pl.pallas_call(functools.partial(_moe_kernel, dims), out_shape=jax.ShapeD...  88.7 us
    pallas_call x1, Pallas kernels, _attn(): pl.pallas_call(functools.partial(_attn_kernel, (b, l, dh, hq, d)), out_sh...  16 us

profile of v4, /device:TPU:0, one launch (start us, length us, event | category | flops | bytes accessed | tf_op | source)
XLA Modules:
  0.0 106.7 jit_solution(2585540687197154845)
XLA Ops:
  0.0 16.0 %attn.1 = (bf16[128,2048]{1,0:T(8,128)(2,1)}, bf16[128,2048]{1,0:T(8,128)(2,1)}, f32[16,128]{1,0:T(8,128)}) custom-call(s32[128]{0:T(128)} %lens.1, bf16[128,2048]{1,0:T(8,128)(2,1)} %x_hbm.1, bf16[2048]{0:T(1024)(128)(2,1)} %ln1.1, bf16[2048]{0:T(1024)(128)(2,1)} %ln2.1, s32[6,128]{1,0:T(8,128)} %bitcast.6, f32[6,128]{1,0:T(8,128)} %bitcast.7, ...), custom_call_target="tpu_custom_call" | custom-call | tf_op jit(solution)/shard_map/attn/pallas_call | solution.py:168
  16.0 88.7 %moe.1 = bf16[128,2048]{1,0:T(8,128)(2,1)} custom-call(bf16[128,2048]{1,0:T(8,128)(2,1)} %get-tuple-element.8.u_ref, bf16[128,2048]{1,0:T(8,128)(2,1)} %get-tuple-element.9.h_ref, f32[16,128]{1,0:T(8,128)} %get-tuple-element.10.rt_ref, bf16[2048,1408]{1,0:T(8,128)(2,1)} %ws1.1, bf16[2048,1408]{1,0:T(8,128)(2,1)} %ws3.1, bf16[1408,2048]{1,0:T(8,128)(2,1)} %ws2.1, ...), custom_call_target="tpu_custom_call" | custom-call | tf_op jit(solution)/shard_map/moe/pallas_call | solution.py:476
  104.8 1.9 %copy.18 = bf16[128,2048]{1,0:T(8,128)(2,1)} copy(bf16[128,2048]{1,0:T(8,128)(2,1)} %moe.1) | data formatting | bytes 1048576

commit v5 on v4

--- a/solution.py
+++ b/solution.py
@@ -20,8 +20,8 @@
 UL = 24
 
 
-def _attn_kernel(dims, lens, x_hbm, ln1, ln2, topk, gates, kk, vv, wq, wo, h_ref, u_ref, rt_ref,
-                 kb, vb, wb, q2, o2, xa, xv, shorts, longs, x_sem, kv_sem, w_sem):
+def _attn_kernel(dims, lens, x_hbm, ln1, ln2, topk, gates, kk, vv, wq, wo, h_hbm, u_hbm, rt_ref,
+                 h_ref, u_ref, out_sem, kb, vb, wb, q2, o2, xa, xv, shorts, longs, x_sem, kv_sem, w_sem):
     b, l, dh, hq, d = dims
     sh = 64
     blk = 2 * sh
@@ -58,25 +58,22 @@
         short = lens[t] <= sh
         shorts[cs] = t
         longs[cl] = t
-
-        @pl.when(short)
-        def _():
-            kv_s(t, cs)
-
-        @pl.when(jnp.logical_not(short))
-        def _():
-            kv_l(t, cl)
-        one = short.astype(jnp.int32)
+        one = (lens[t] <= sh).astype(jnp.int32)
         return cs + one, cl + 1 - one
-    ns, nl = lax.fori_loop(0, b, sort_rows, (0, 0))
-    odd = lax.rem(ns, 2)
-
-    @pl.when(odd == 1)
-    def _():
-        kv_s(shorts[ns - 1], ns)
+    ns, nl = lax.fori_loop(0, b, sort_rows, (0, 0), unroll=4)
     last = shorts[jnp.maximum(ns - 1, 0)]
     shorts[ns] = last
-    ns2 = ns + odd
+    ns2 = ns + lax.rem(ns, 2)
+
+    def issue_s(i, carry):
+        kv_s(shorts[i], i)
+        return carry
+    lax.fori_loop(0, ns2, issue_s, 0)
+
+    def issue_l(i, carry):
+        kv_l(longs[i], i)
+        return carry
+    lax.fori_loop(0, nl, issue_l, 0)
 
     k = topk.shape[0]
     rt_ref[...] = jnp.concatenate(
@@ -143,18 +140,27 @@
 
     for hh in range(hq):
         xa[:, hh * dh:(hh + 1) * dh] = o2[pl.ds(hh, b, stride=hq), :].astype(BF)
+    def out(src, dst, j, q):
+        cs = pl.ds(j * cq, cq)
+        return pltpu.make_async_copy(src.at[:, cs], dst.at[:, cs], out_sem.at[q, j])
+
     ssq = jnp.zeros((b, 1), F32)
     for j in range(4):
         cs = slice(j * cq, (j + 1) * cq)
         wcopy(wo, j, 1).wait()
         hv = (xv[:, cs].astype(F32) + jnp.dot(xa[...], wb[:, cs], preferred_element_type=F32)).astype(BF)
         h_ref[:, cs] = hv
+        out(h_ref, h_hbm, j, 0).start()
         hf = hv.astype(F32)
         ssq += jnp.sum(hf * hf, axis=-1, keepdims=True)
     r = lax.rsqrt(ssq * (1.0 / d) + EPS)
     for j in range(4):
         cs = slice(j * cq, (j + 1) * cq)
         u_ref[:, cs] = (h_ref[:, cs].astype(F32) * r * ln2[cs].astype(F32).reshape(1, cq)).astype(BF)
+        out(u_ref, u_hbm, j, 1).start()
+    for j in range(4):
+        out(h_ref, h_hbm, j, 0).wait()
+        out(u_ref, u_hbm, j, 1).wait()
 
 
 def _attn(x, kk, vv, lens, ln1, ln2, topk, gates, wq, wo):
@@ -170,8 +176,9 @@
         out_shape=(jax.ShapeDtypeStruct((b, d), BF), jax.ShapeDtypeStruct((b, d), BF),
                    jax.ShapeDtypeStruct((16, b), F32)),
         in_specs=[pl.BlockSpec(memory_space=pltpu.SMEM), anys, vm, vm, vm, vm, anys, anys, anys, anys],
-        out_specs=(vm, vm, vm),
+        out_specs=(anys, anys, vm),
         scratch_shapes=[
+            pltpu.VMEM((b, d), BF), pltpu.VMEM((b, d), BF), dma((2, 4)),
             pltpu.VMEM((b * l, dh), BF), pltpu.VMEM((b * l, dh), BF), pltpu.VMEM((d, d), BF),
             pltpu.VMEM((b * hq, dh), F32), pltpu.VMEM((b * hq, dh), F32),
             pltpu.VMEM((b, d), BF), pltpu.VMEM((b, d), BF),
@@ -261,7 +268,7 @@
     for i in range(1, 8):
         rts(i).start()
     for k in range(nk):
-        for j in range(4):
+        for j in (2, 0, 1, 3):
             ag(k, j).start()
 
     def swiglu(g, v):
@@ -417,10 +424,6 @@
         @pl.when(n > 1)
         def _():
             stage2(n - 2)
-
-        @pl.when(n == nn // 2)
-        def _():
-            pass
         return carry
     lax.fori_loop(0, nn, block, 0)
     stage1(nn - 1)
@@ -445,10 +448,18 @@
         base[n] += hv[:, n * NC:(n + 1) * NC].astype(F32) + sh
         if n + NB < nn:
             copy_b(t + NB, n + NB, None).start()
+
+    def out(n):
+        cs = pl.ds(n * NC, NC)
+        return pltpu.make_async_copy(hv.at[:, cs], y_ref.at[:, cs], b_sem.at[n])
+
     for n in range(nn):
         send_a(n).wait_recv()
         send_b(n).wait_recv()
-        y_ref[:, n * NC:(n + 1) * NC] = (base[n] + r_a[n] + r_b[n]).astype(BF)
+        hv[:, n * NC:(n + 1) * NC] = (base[n] + r_a[n] + r_b[n]).astype(BF)
+        out(n).start()
+    for n in range(nn):
+        out(n).wait()
     for i in range(1, 8):
         rts(i).wait_send()
     for k in range(nk):
@@ -477,7 +488,7 @@
         functools.partial(_moe_kernel, dims),
         out_shape=jax.ShapeDtypeStruct((b, d), BF),
         in_specs=[anys] * 9,
-        out_specs=pl.BlockSpec(memory_space=pltpu.VMEM),
+        out_specs=anys,
         scratch_shapes=[
             pltpu.VMEM((8 * b, d), BF),
             pltpu.VMEM((8, 16, b), F32),

time: 107 us -> 104 us (0.972)
  Pallas kernels: 105 us -> 102 us
    pallas_call x1, Pallas kernels: 88.7 us -> 87.2 us  [_moe(): pl.pallas_call(functools.partial(_moe_kernel, dims), out_shape=jax.ShapeD...]
where the time goes in v5:
time: 104 us
  Pallas kernels  102 us (98%)
  local copies, waits for them, and re-layouts  1.88 us (2%)
    pallas_call x1, Pallas kernels, _moe(): pl.pallas_call(functools.partial(_moe_kernel, dims), out_shape=jax.ShapeD...  87.2 us
    pallas_call x1, Pallas kernels, _attn(): pl.pallas_call(functools.partial(_attn_kernel, (b, l, dh, hq, d)), out_sh...  15 us

profile of v5, /device:TPU:0, one launch (start us, length us, event | category | flops | bytes accessed | tf_op | source)
XLA Modules:
  0.0 104.2 jit_solution(2295980962323434172)
XLA Ops:
  0.0 15.0 %attn.1 = (bf16[128,2048]{1,0:T(8,128)(2,1)}, bf16[128,2048]{1,0:T(8,128)(2,1)}, f32[16,128]{1,0:T(8,128)}) custom-call(s32[128]{0:T(128)} %lens.1, bf16[128,2048]{1,0:T(8,128)(2,1)} %x_hbm.1, bf16[2048]{0:T(1024)(128)(2,1)} %ln1.1, bf16[2048]{0:T(1024)(128)(2,1)} %ln2.1, s32[6,128]{1,0:T(8,128)} %bitcast.6, f32[6,128]{1,0:T(8,128)} %bitcast.7, ...), custom_call_target="tpu_custom_call" | custom-call | tf_op jit(solution)/shard_map/attn/pallas_call | solution.py:174
  15.0 87.2 %moe.1 = bf16[128,2048]{1,0:T(8,128)(2,1)} custom-call(bf16[128,2048]{1,0:T(8,128)(2,1)} %get-tuple-element.8.u_ref, bf16[128,2048]{1,0:T(8,128)(2,1)} %get-tuple-element.9.h_ref, f32[16,128]{1,0:T(8,128)} %get-tuple-element.10.rt_ref, bf16[2048,1408]{1,0:T(8,128)(2,1)} %ws1.1, bf16[2048,1408]{1,0:T(8,128)(2,1)} %ws3.1, bf16[1408,2048]{1,0:T(8,128)(2,1)} %ws2.1, ...), custom_call_target="tpu_custom_call" | custom-call | tf_op jit(solution)/shard_map/moe/pallas_call | solution.py:487
  102.3 1.9 %copy.18 = bf16[128,2048]{1,0:T(8,128)(2,1)} copy(bf16[128,2048]{1,0:T(8,128)(2,1)} %moe.1) | data formatting | bytes 1048576

commit v6 on v5

--- a/solution.py
+++ b/solution.py
@@ -311,7 +311,7 @@
         pg[p, 4 * b:6 * b, :] = lo
 
     def forward(k):
-        for j in range(3):
+        for j in (2, 0, 1):
             ag(k, j).wait_recv()
             fw(k, j).start()
 

time: 104 us -> 104 us (level)
    pallas_call x1, Pallas kernels: 87.2 us -> 86.1 us  [_moe(): pl.pallas_call(functools.partial(_moe_kernel, dims), out_shape=jax.ShapeD...]
where the time goes in v6:
time: 104 us; the launch traced here: 103 us
  Pallas kernels  101 us (97%)
  local copies, waits for them, and re-layouts  1.88 us (2%)
    pallas_call x1, Pallas kernels, _moe(): pl.pallas_call(functools.partial(_moe_kernel, dims), out_shape=jax.ShapeD...  86.1 us
    pallas_call x1, Pallas kernels, _attn(): pl.pallas_call(functools.partial(_attn_kernel, (b, l, dh, hq, d)), out_sh...  15.2 us

profile of v6, /device:TPU:0, one launch (start us, length us, event | category | flops | bytes accessed | tf_op | source)
XLA Modules:
  0.0 103.2 jit_solution(7447598472406841605)
XLA Ops:
  0.0 15.2 %attn.1 = (bf16[128,2048]{1,0:T(8,128)(2,1)}, bf16[128,2048]{1,0:T(8,128)(2,1)}, f32[16,128]{1,0:T(8,128)}) custom-call(s32[128]{0:T(128)} %lens.1, bf16[128,2048]{1,0:T(8,128)(2,1)} %x_hbm.1, bf16[2048]{0:T(1024)(128)(2,1)} %ln1.1, bf16[2048]{0:T(1024)(128)(2,1)} %ln2.1, s32[6,128]{1,0:T(8,128)} %bitcast.6, f32[6,128]{1,0:T(8,128)} %bitcast.7, ...), custom_call_target="tpu_custom_call" | custom-call | tf_op jit(solution)/shard_map/attn/pallas_call | solution.py:174
  15.2 86.1 %moe.1 = bf16[128,2048]{1,0:T(8,128)(2,1)} custom-call(bf16[128,2048]{1,0:T(8,128)(2,1)} %get-tuple-element.8.u_ref, bf16[128,2048]{1,0:T(8,128)(2,1)} %get-tuple-element.9.h_ref, f32[16,128]{1,0:T(8,128)} %get-tuple-element.10.rt_ref, bf16[2048,1408]{1,0:T(8,128)(2,1)} %ws1.1, bf16[2048,1408]{1,0:T(8,128)(2,1)} %ws3.1, bf16[1408,2048]{1,0:T(8,128)(2,1)} %ws2.1, ...), custom_call_target="tpu_custom_call" | custom-call | tf_op jit(solution)/shard_map/moe/pallas_call | solution.py:487
  101.3 1.9 %copy.18 = bf16[128,2048]{1,0:T(8,128)(2,1)} copy(bf16[128,2048]{1,0:T(8,128)(2,1)} %moe.1) | data formatting | bytes 1048576
